TPU v7x, 256 devices: a 4x2x16 block of a 4x16x16 slice. The times are simulated.
256 devices in a mesh: member: 2 (over y), lat: 128 (over z, x, core).
Axes of the slice: x: 4, y: 2, z: 16, core: 2. Of those that a mesh axis runs over, the one named last changes fastest.
The devices are a block of a 4x16x16 slice.
Arguments:
- tracers: float32 [60, 4, 512, 1440], P('member', None, 'lat'), parts along dimension 0, may hold values from -6 to 6
- currents: float32 [4, 4, 512, 1440], P('member', None, 'lat'), parts along dimension 0, may hold values from -0.4 to 0.4
- column_levels: int32 [1024, 1440], P(('member', 'lat')), parts along dimension 0, may hold values from 0 to 4
Outputs:
- advected: float32 [60, 4, 512, 1440], P('member', None, 'lat'), parts along dimension 0
There are 2 independent parts, one for each index of `member`. A program takes and returns all parts, laid end to end along the dimension named above; each array names one. Nothing has to cross between parts.
All inputs are finite; a program needn't handle non-finite values.
Results may differ from a plain program's by a relative error of at most 0.00002.
Values sent between devices are 32-bit elements; how exact they have to be, the bound alone decides.
No kernel may reach another device: no remote copies, remote signals or barrier semaphores. Data moves between devices by JAX's collectives and lax.ppermute only.
A program may use at most 64 MiB of HBM per device.

v0:
```python
import jax
import jax.numpy as jnp
from jax import lax
from jax.sharding import PartitionSpec as P


def extended(block, sides, width):
    for axis, dim in sides:
        count = lax.axis_size(axis)
        forward = [(i, i + 1) for i in range(count - 1)]
        backward = [(target, source) for source, target in forward]
        low = lax.ppermute(
            lax.slice_in_dim(block, block.shape[dim] - width, None, axis=dim), axis, forward
        )
        high = lax.ppermute(lax.slice_in_dim(block, 0, width, axis=dim), axis, backward)
        block = jnp.concatenate([low, block, high], axis=dim)
    return block


def face_flux(courant, before, left, right, after):
    central = courant * (7.0 * (left + right) - (before + after)) / 12.0
    upwind = jnp.abs(courant) * (3.0 * (right - left) - (after - before)) / 12.0
    return central - upwind


def advect_section(padded, east_pad, north_pad, wet_pad):
    rows = padded.shape[-2] - 4
    field = padded[..., 2:-2, :]
    east = east_pad[:, 1:-1]
    wet_rows = wet_pad[:, 1:-1]
    east_face = 0.5 * (east + jnp.roll(east, -1, -1))
    east_open = wet_rows * jnp.roll(wet_rows, -1, -1)
    east_flux = east_open * face_flux(
        east_face, jnp.roll(field, 1, -1), field, jnp.roll(field, -1, -1), jnp.roll(field, -2, -1)
    )
    east_div = east_flux - jnp.roll(east_flux, 1, -1)
    north_face = 0.5 * (north_pad[:, :-1] + north_pad[:, 1:])
    north_open = wet_pad[:, :-1] * wet_pad[:, 1:]
    north_flux = north_open * face_flux(
        north_face,
        padded[..., 0 : rows + 1, :],
        padded[..., 1 : rows + 2, :],
        padded[..., 2 : rows + 3, :],
        padded[..., 3 : rows + 4, :],
    )
    north_div = north_flux[..., 1:, :] - north_flux[..., :-1, :]
    return field - east_div - north_div


def north_fold(padded, width, factor, is_top):
    inner = padded.shape[-2] - 2 * width
    source = padded[..., inner : inner + width, :]
    ghost = factor * jnp.flip(source, axis=(-2, -1))
    folded = jnp.concatenate([padded[..., : width + inner, :], ghost], axis=-2)
    return jnp.where(is_top, folded, padded)


def tracer_pad(field, is_top):
    padded = extended(field, (("lat", 2),), 2)
    return north_fold(padded, 2, 1.0, is_top)


def shards(tracers, currents, column_levels):
    is_top = lax.axis_index("lat") == lax.axis_size("lat") - 1
    levels = jnp.arange(tracers.shape[1], dtype=jnp.int32)
    wet = (levels[:, None, None] < column_levels[None]).astype(jnp.float32)
    flow = jnp.concatenate([currents, wet[None]], axis=0)
    factors = jnp.array([-1.0, -1.0, 1.0], jnp.float32)[:, None, None, None]
    start = tracers * wet
    flow_pad = extended(flow, (("lat", 2),), 1)
    flow_pad = north_fold(flow_pad, 1, factors, is_top)
    first = advect_section(tracer_pad(start, is_top), flow_pad[0], flow_pad[1], flow_pad[2]) * wet
    second = advect_section(tracer_pad(first, is_top), flow_pad[0], flow_pad[1], flow_pad[2])
    return 0.5 * (start + second) * wet


def solution(mesh):
    in_specs = (
        P("member", None, "lat", None),
        P("member", None, "lat", None),
        P(("member", "lat"), None),
    )
    out_specs = P("member", None, "lat", None)
    return jax.shard_map(shards, mesh=mesh, in_specs=in_specs, out_specs=out_specs, check_vma=False)
```

profile of v0, /device:TPU:33, one launch (start us, length us, event | category | flops | bytes accessed | tf_op | source)
XLA Modules:
  0.0 122.6 jit_solution(7482346235792889461)
XLA Ops:
  0.0 0.8 fusion.11
  0.8 1.8 %pad_maximum_fusion.8 = (f32[3,4,1,1440]{3,2,1,0:T(1,128)}, f32[3,4,1,1440]{3,2,1,0:T(1,128)S(1)}) fusion(f32[1,4,4,1440]{3,2,1,0:T(4,128)S(1)} %fusion.11, f32[2,4,4,1440]{3,2,1,0:T(4,128)} %param.5), kind=kLoop, calls=%fused_computation.42 | loop fusion | flops 34560 | bytes 414720 | tf_op jit(solution)/shard_map/concatenate | solution.py:67
  2.5 4.6 %collective-permute-start.2 = (f32[3,4,1,1440]{3,2,1,0:T(1,128)S(1)}, f32[3,4,1,1440]{3,2,1,0:T(1,128)}, u32[]{:S(2)}, u32[]{:S(2)}) collective-permute-start(f32[3,4,1,1440]{3,2,1,0:T(1,128)S(1)} %get-tuple-element.25), channel_id=1, source_target_pairs={{0,1},{1,2},{2,3},{3,4},{4,5},{5,6},{6,7},{7,8},{8,9},{9,10},{10,1... | collective-permute-start | bytes 207368 | tf_op jit(solution)/shard_map/ppermute | solution.py:12
  7.1 19.7 %collective-permute-start.3 = (f32[3,4,1,1440]{3,2,1,0:T(1,128)}, f32[3,4,1,1440]{3,2,1,0:T(1,128)}, u32[]{:S(2)}, u32[]{:S(2)}) collective-permute-start(f32[3,4,1,1440]{3,2,1,0:T(1,128)} %get-tuple-element.24), channel_id=1, source_target_pairs={{1,0},{2,1},{3,2},{4,3},{5,4},{6,5},{7,6},{8,7},{9,8},{10,9},{11,1... | collective-permute-start | bytes 207368 | tf_op jit(solution)/shard_map/ppermute | solution.py:15
  26.8 0.8 fusion.10
  27.6 3.1 %copy_multiply_fusion = f32[30,4,4,1440]{3,1,2,0:T(4,128)S(1)} fusion(f32[30,4,4,1440]{3,2,1,0:T(4,128)} %param.4, f32[4,4,1440]{2,0,1:T(4,128)S(1)} %copy.5), kind=kLoop, calls=%fused_computation.23 | loop fusion | flops 691200 | bytes 5621760 | tf_op jit(solution)/shard_map/mul | solution.py:69
  30.7 0.0 copy-start.9
  30.7 1.8 %fusion.21 = (f32[30,4,2,1440]{3,1,2,0:T(4,128)}, f32[30,4,2,1440]{3,1,2,0:T(4,128)}) fusion(f32[30,4,4,1440]{3,1,2,0:T(4,128)S(1)} %copy_multiply_fusion), kind=kLoop, calls=%fused_computation.52 | loop fusion | bytes 5529600 | tf_op jit(solution)/shard_map/slice | solution.py:15
  32.5 1.9 %collective-permute-start = (f32[30,4,2,1440]{3,1,2,0:T(4,128)}, f32[30,4,2,1440]{3,1,2,0:T(4,128)}, u32[]{:S(2)}, u32[]{:S(2)}) collective-permute-start(f32[30,4,2,1440]{3,1,2,0:T(4,128)} %get-tuple-element.20), channel_id=1, source_target_pairs={{0,1},{1,2},{2,3},{3,4},{4,5},{5,6},{6,7},{7,8},{8,9},{9,10},{10,1... | collective-permute-start | bytes 4147208 | tf_op jit(solution)/shard_map/ppermute | solution.py:12
  34.5 3.8 %collective-permute-start.1 = (f32[30,4,2,1440]{3,1,2,0:T(4,128)}, f32[30,4,2,1440]{3,1,2,0:T(4,128)}, u32[]{:S(2)}, u32[]{:S(2)}) collective-permute-start(f32[30,4,2,1440]{3,1,2,0:T(4,128)} %get-tuple-element.19), channel_id=1, source_target_pairs={{1,0},{2,1},{3,2},{4,3},{5,4},{6,5},{7,6},{8,7},{9,8},{10,9},{11,1... | collective-permute-start | bytes 4147208 | tf_op jit(solution)/shard_map/ppermute | solution.py:15
  38.2 1.6 %reverse.1 = f32[3,4,1,1536]{3,2,1,0:T(1,128)S(1)} reverse(f32[3,4,1,1536]{3,2,1,0:T(1,128)S(1)} %bitcast.13), dimensions={2,3} | reverse | bytes 147456
  39.9 0.0 copy-done.9
  39.9 0.2 broadcast_multiply_fusion
  40.1 0.0 copy-start.6
  40.1 8.2 %reverse = f32[30,4,2,1536]{3,1,2,0:T(4,128)} reverse(f32[30,4,2,1536]{3,1,2,0:T(4,128)} %bitcast.6), dimensions={2,3} | reverse | bytes 2949120
  48.3 3.3 %slice.328 = f32[30,4,2,1440]{3,1,2,0:T(4,128)} slice(f32[30,4,2,1536]{3,1,2,0:T(4,128)} %reverse), slice={[0:30], [0:4], [0:2], [96:1536]} | slice | bytes 2764800
  51.6 0.0 collective-permute-done.2
  51.7 0.0 collective-permute-done.3
  51.7 0.0 copy-done.6
  51.7 1.3 %maximum_select_fusion.2 = f32[3,4,6,1440]{3,2,1,0:T(8,128)S(1)} fusion(f32[3,4,1,1440]{3,2,1,0:T(1,128)S(1)} %broadcast_multiply_fusion, f32[1,4,4,1440]{3,2,1,0:T(4,128)S(1)} %fusion.11, f32[2,4,4,1440]{3,2,1,0:T(4,128)S(1)} %copy-done.6, f32[3,4,1,1440]{3,2,1,0:T(1,128)} %collective-permute-done.2, f32[3,4,1,1440]{3,2,1,0:T(1,128)} %collective-permute-done.3, ...), kind=kLoop, calls=%fused_computation.26 | loop fusion | flops 518400 | bytes 898561 | tf_op jit(solution)/shard_map/jit(_where)/select_n | solution.py:55
  53.1 0.1 slice.247
  53.2 0.1 slice.251
  53.3 0.1 slice_multiply_fusion.1
  53.5 0.1 fusion.12
  53.6 0.0 copy-start.2
  53.6 0.0 copy-start.4
  53.7 0.1 copy.10
  53.8 0.1 copy.11
  53.9 0.1 copy.12
  54.0 0.0 collective-permute-done
  54.0 1.5 %collective-permute-done.1 = f32[30,4,2,1440]{3,1,2,0:T(4,128)} collective-permute-done((f32[30,4,2,1440]{3,1,2,0:T(4,128)}, f32[30,4,2,1440]{3,1,2,0:T(4,128)}, u32[]{:S(2)}, u32[]{:S(2)}) %collective-permute-start.1) | collective-permute-done | bytes 1382432 | tf_op jit(solution)/shard_map/ppermute | solution.py:15
  55.5 0.0 copy-done.1
  55.5 3.4 %maximum_select_fusion = f32[30,4,8,1440]{3,1,2,0:T(4,128)S(1)} fusion(f32[30,4,2,1440]{3,1,2,0:T(4,128)S(1)} %copy-done.1, f32[30,4,4,1440]{3,1,2,0:T(4,128)S(1)} %copy_multiply_fusion, f32[30,4,2,1440]{3,1,2,0:T(4,128)} %collective-permute-done, f32[30,4,2,1440]{3,1,2,0:T(4,128)} %collective-permute-done.1, pred[]{:T(512)S(6)} %eq.3), kind=kLoop, calls=%fused_computation | loop fusion | flops 5529600 | bytes 12441601 | tf_op jit(solution)/shard_map/jit(_where)/select_n | solution.py:55
  59.0 1.9 %fusion.18 = (f32[30,4,4,1439]{3,1,2,0:T(4,128)S(1)}, f32[30,4,4,1439]{3,1,2,0:T(4,128)S(1)}) fusion(f32[30,4,8,1440]{3,1,2,0:T(4,128)S(1)} %maximum_select_fusion), kind=kLoop, calls=%fused_computation.49 | loop fusion | bytes 11051520 | tf_op jit(solution)/shard_map/jit(_roll_static)/slice | solution.py:34
  60.9 0.2 fusion.19
  61.1 1.6 %slice.257 = f32[30,4,4,1438]{3,1,2,0:T(4,128)S(1)} slice(f32[30,4,8,1440]{3,1,2,0:T(4,128)S(1)} %maximum_select_fusion), slice={[0:30], [0:4], [2:6], [2:1440]} | slice | bytes 5521920 | tf_op jit(solution)/shard_map/jit(_roll_static)/slice | solution.py:34
  62.7 0.0 copy-done.2
  62.7 0.0 copy-done.4
  62.7 4.8 %subtract_multiply_fusion.3 = f32[30,4,4,1440]{3,1,2,0:T(4,128)S(1)} fusion(f32[30,4,4,2]{3,1,2,0:T(4,128)S(1)} %slice.258, f32[30,4,4,1438]{3,1,2,0:T(4,128)S(1)} %slice.257, f32[30,4,4,1439]{3,1,2,0:T(4,128)S(1)} %get-tuple-element.14, f32[30,4,4,1]{3,1,2,0:T(4,128)S(1)} %get-tuple-element.16, f32[30,4,4,1]{3,1,2,0:T(4,128)S(1)} %get-tuple-element.15, ...), kind=kLoop, calls=%fused_computation.25 | loop fusion | flops 11750400 | bytes 14100480 | tf_op jit(solution)/shard_map/mul | solution.py:33
  67.5 0.2 slice.259
  67.7 3.8 %subtract_multiply_fusion.1 = f32[30,4,5,1440]{3,1,2,0:T(4,128)S(1)} fusion(f32[30,4,8,1440]{3,1,2,0:T(4,128)S(1)} %maximum_select_fusion, f32[4,5,1440]{2,0,1:T(4,128)S(1)} %copy.12, f32[4,5,1440]{2,0,1:T(4,128)S(1)} %copy.11, f32[4,5,1440]{2,0,1:T(4,128)S(1)} %copy.10), kind=kLoop, calls=%fused_computation.5 | loop fusion | flops 12096000 | bytes 17625600 | tf_op jit(solution)/shard_map/mul | solution.py:39
  71.5 2.8 %fusion.4 = f32[30,4,4,1440]{3,1,2,0:T(4,128)S(1)} fusion(f32[30,4,5,1440]{3,1,2,0:T(4,128)S(1)} %subtract_multiply_fusion.1, f32[30,4,4,1440]{3,1,2,0:T(4,128)S(1)} %subtract_multiply_fusion.3, f32[30,4,4,1439]{3,1,2,0:T(4,128)S(1)} %bitcast.11, f32[30,4,4,1]{3,1,2,0:T(4,128)S(1)} %slice.259, f32[30,4,8,1440]{3,1,2,0:T(4,128)S(1)} %maximum_select_fusion, ...), kind=kLoop, calls=%fused_computation.12 | loop fusion | flops 4147200 | bytes 16680960 | tf_op jit(solution)/shard_map/mul | solution.py:72
  74.4 0.0 copy-start.8
  74.4 1.9 %fusion.20 = (f32[30,4,2,1440]{3,1,2,0:T(4,128)}, f32[30,4,2,1440]{3,1,2,0:T(4,128)}) fusion(f32[30,4,4,1440]{3,1,2,0:T(4,128)S(1)} %fusion.4), kind=kLoop, calls=%fused_computation.51 | loop fusion | bytes 5529600 | tf_op jit(solution)/shard_map/slice | solution.py:15
  76.2 1.9 %collective-permute-start.4 = (f32[30,4,2,1440]{3,1,2,0:T(4,128)}, f32[30,4,2,1440]{3,1,2,0:T(4,128)}, u32[]{:S(2)}, u32[]{:S(2)}) collective-permute-start(f32[30,4,2,1440]{3,1,2,0:T(4,128)} %get-tuple-element.18), channel_id=1, source_target_pairs={{0,1},{1,2},{2,3},{3,4},{4,5},{5,6},{6,7},{7,8},{8,9},{9,10},{10,1... | collective-permute-start | bytes 4147208 | tf_op jit(solution)/shard_map/ppermute | solution.py:12
  78.2 3.8 %collective-permute-start.5 = (f32[30,4,2,1440]{3,1,2,0:T(4,128)}, f32[30,4,2,1440]{3,1,2,0:T(4,128)}, u32[]{:S(2)}, u32[]{:S(2)}) collective-permute-start(f32[30,4,2,1440]{3,1,2,0:T(4,128)} %get-tuple-element.17), channel_id=1, source_target_pairs={{1,0},{2,1},{3,2},{4,3},{5,4},{6,5},{7,6},{8,7},{9,8},{10,9},{11,1... | collective-permute-start | bytes 4147208 | tf_op jit(solution)/shard_map/ppermute | solution.py:15
  82.0 0.0 copy-done.8
  82.0 0.7 copy.13
  82.7 8.2 %reverse.2 = f32[30,4,2,1536]{3,1,2,0:T(4,128)} reverse(f32[30,4,2,1536]{3,1,2,0:T(4,128)} %bitcast.8), dimensions={2,3} | reverse | bytes 2949120
  90.8 2.2 %slice.330 = f32[30,4,2,1440]{3,1,2,0:T(4,128)S(1)} slice(f32[30,4,2,1536]{3,1,2,0:T(4,128)} %reverse.2), slice={[0:30], [0:4], [0:2], [96:1536]} | slice | bytes 2764800
  93.0 1.7 %collective-permute-done.4 = f32[30,4,2,1440]{3,1,2,0:T(4,128)} collective-permute-done((f32[30,4,2,1440]{3,1,2,0:T(4,128)}, f32[30,4,2,1440]{3,1,2,0:T(4,128)}, u32[]{:S(2)}, u32[]{:S(2)}) %collective-permute-start.4) | collective-permute-done | bytes 1382432 | tf_op jit(solution)/shard_map/ppermute | solution.py:12
  94.8 4.4 %collective-permute-done.5 = f32[30,4,2,1440]{3,1,2,0:T(4,128)} collective-permute-done((f32[30,4,2,1440]{3,1,2,0:T(4,128)}, f32[30,4,2,1440]{3,1,2,0:T(4,128)}, u32[]{:S(2)}, u32[]{:S(2)}) %collective-permute-start.5) | collective-permute-done | bytes 1382432 | tf_op jit(solution)/shard_map/ppermute | solution.py:15
  99.2 3.4 %maximum_select_fusion.1 = f32[30,4,8,1440]{3,1,2,0:T(4,128)S(1)} fusion(f32[30,4,2,1440]{3,1,2,0:T(4,128)S(1)} %slice.330, f32[30,4,4,1440]{3,1,2,0:T(4,128)S(1)} %fusion.4, f32[30,4,2,1440]{3,1,2,0:T(4,128)} %collective-permute-done.4, f32[30,4,2,1440]{3,1,2,0:T(4,128)} %collective-permute-done.5, pred[]{:T(512)S(6)} %eq.3), kind=kLoop, calls=%fused_computation.2 | loop fusion | flops 5529600 | bytes 12441601 | tf_op jit(solution)/shard_map/jit(_where)/select_n | solution.py:55
  102.7 1.9 %fusion.16 = (f32[30,4,4,1439]{3,1,2,0:T(4,128)S(1)}, f32[30,4,4,1439]{3,1,2,0:T(4,128)S(1)}) fusion(f32[30,4,8,1440]{3,1,2,0:T(4,128)S(1)} %maximum_select_fusion.1), kind=kLoop, calls=%fused_computation.47 | loop fusion | bytes 11051520 | tf_op jit(solution)/shard_map/jit(_roll_static)/slice | solution.py:34
  104.6 1.6 %slice.279 = f32[30,4,4,1438]{3,1,2,0:T(4,128)S(1)} slice(f32[30,4,8,1440]{3,1,2,0:T(4,128)S(1)} %maximum_select_fusion.1), slice={[0:30], [0:4], [2:6], [2:1440]} | slice | bytes 5521920 | tf_op jit(solution)/shard_map/jit(_roll_static)/slice | solution.py:34
  106.2 0.2 fusion.17
  106.4 3.8 %subtract_multiply_fusion = f32[30,4,5,1440]{3,1,2,0:T(4,128)S(1)} fusion(f32[30,4,8,1440]{3,1,2,0:T(4,128)S(1)} %maximum_select_fusion.1, f32[4,5,1440]{2,0,1:T(4,128)S(1)} %copy.12, f32[4,5,1440]{2,0,1:T(4,128)S(1)} %copy.11, f32[4,5,1440]{2,0,1:T(4,128)S(1)} %copy.10), kind=kLoop, calls=%fused_computation.4 | loop fusion | flops 12096000 | bytes 17625600 | tf_op jit(solution)/shard_map/mul | solution.py:39
  110.3 0.0 copy-start
  110.3 0.0 copy-start.7
  110.3 4.8 %subtract_multiply_fusion.2 = f32[30,4,4,1440]{3,1,2,0:T(4,128)S(1)} fusion(f32[30,4,4,2]{3,1,2,0:T(4,128)S(1)} %slice.280, f32[30,4,4,1438]{3,1,2,0:T(4,128)S(1)} %slice.279, f32[30,4,4,1439]{3,1,2,0:T(4,128)S(1)} %get-tuple-element.10, f32[30,4,4,1]{3,1,2,0:T(4,128)S(1)} %get-tuple-element.12, f32[30,4,4,1]{3,1,2,0:T(4,128)S(1)} %get-tuple-element.11, ...), kind=kLoop, calls=%fused_computation.24 | loop fusion | flops 11750400 | bytes 14100480 | tf_op jit(solution)/shard_map/mul | solution.py:33
  115.1 0.2 slice.281
  115.3 0.0 copy-done
  115.3 4.5 %fusion.2 = f32[30,4,4,1440]{3,1,2,0:T(4,128)S(1)} fusion(f32[30,4,5,1440]{3,1,2,0:T(4,128)S(1)} %subtract_multiply_fusion, f32[30,4,4,1440]{3,1,2,0:T(4,128)S(1)} %subtract_multiply_fusion.2, f32[30,4,4,1439]{3,1,2,0:T(4,128)S(1)} %bitcast.12, f32[30,4,4,1]{3,1,2,0:T(4,128)S(1)} %slice.281, f32[30,4,8,1440]{3,1,2,0:T(4,128)S(1)} %maximum_select_fusion.1, ...), kind=kLoop, calls=%fused_computation.9 | loop fusion | flops 5529600 | bytes 19537920 | tf_op jit(solution)/shard_map/mul | solution.py:74
  119.8 2.7 %copy.14 = f32[30,4,4,1440]{3,2,1,0:T(4,128)} copy(f32[30,4,4,1440]{3,1,2,0:T(4,128)S(1)} %fusion.2) | data formatting | bytes 5529600 | tf_op jit(solution)/shard_map/mul | solution.py:74
  (18 shorter events, 0.4 us)
Async XLA Ops:
  2.5 49.1 %collective-permute-start.2 = (f32[3,4,1,1440]{3,2,1,0:T(1,128)S(1)}, f32[3,4,1,1440]{3,2,1,0:T(1,128)}, u32[]{:S(2)}, u32[]{:S(2)}) collective-permute-start(f32[3,4,1,1440]{3,2,1,0:T(1,128)S(1)} %get-tuple-element.25), channel_id=1, source_target_pairs={{0,1},{1,2},{2,3},{3,4},{4,5},{5,6},{6,7},{7,8},{8,9},{9,10},{10,1... | collective-permute-start | bytes 207368 | tf_op jit(solution)/shard_map/ppermute | solution.py:12
  7.1 44.5 %collective-permute-start.3 = (f32[3,4,1,1440]{3,2,1,0:T(1,128)}, f32[3,4,1,1440]{3,2,1,0:T(1,128)}, u32[]{:S(2)}, u32[]{:S(2)}) collective-permute-start(f32[3,4,1,1440]{3,2,1,0:T(1,128)} %get-tuple-element.24), channel_id=1, source_target_pairs={{1,0},{2,1},{3,2},{4,3},{5,4},{6,5},{7,6},{8,7},{9,8},{10,9},{11,1... | collective-permute-start | bytes 207368 | tf_op jit(solution)/shard_map/ppermute | solution.py:15
  30.7 9.2 %copy-start.9 = (f32[3]{0:T(128)S(1)}, f32[3]{0:T(128)}, u32[]{:S(2)}) copy-start(f32[3]{0:T(128)} %constant.31.clone) | copy-start | bytes 40
  32.5 21.5 %collective-permute-start = (f32[30,4,2,1440]{3,1,2,0:T(4,128)}, f32[30,4,2,1440]{3,1,2,0:T(4,128)}, u32[]{:S(2)}, u32[]{:S(2)}) collective-permute-start(f32[30,4,2,1440]{3,1,2,0:T(4,128)} %get-tuple-element.20), channel_id=1, source_target_pairs={{0,1},{1,2},{2,3},{3,4},{4,5},{5,6},{6,7},{7,8},{8,9},{9,10},{10,1... | collective-permute-start | bytes 4147208 | tf_op jit(solution)/shard_map/ppermute | solution.py:12
  34.5 21.0 %collective-permute-start.1 = (f32[30,4,2,1440]{3,1,2,0:T(4,128)}, f32[30,4,2,1440]{3,1,2,0:T(4,128)}, u32[]{:S(2)}, u32[]{:S(2)}) collective-permute-start(f32[30,4,2,1440]{3,1,2,0:T(4,128)} %get-tuple-element.19), channel_id=1, source_target_pairs={{1,0},{2,1},{3,2},{4,3},{5,4},{6,5},{7,6},{8,7},{9,8},{10,9},{11,1... | collective-permute-start | bytes 4147208 | tf_op jit(solution)/shard_map/ppermute | solution.py:15
  40.1 11.6 %copy-start.6 = (f32[2,4,4,1440]{3,2,1,0:T(4,128)S(1)}, f32[2,4,4,1440]{3,2,1,0:T(4,128)}, u32[]{:S(2)}) copy-start(f32[2,4,4,1440]{3,2,1,0:T(4,128)} %param.5) | copy-start | bytes 552964
  51.6 3.9 %copy-start.1 = (f32[30,4,2,1440]{3,1,2,0:T(4,128)S(1)}, f32[30,4,2,1440]{3,1,2,0:T(4,128)}, u32[]{:S(2)}) copy-start(f32[30,4,2,1440]{3,1,2,0:T(4,128)} %slice.328) | copy-start | bytes 4147204
  53.6 9.1 %copy-start.2 = (f32[4,4,1440]{2,0,1:T(4,128)}, f32[4,4,1440]{2,0,1:T(4,128)S(1)}, u32[]{:S(2)}) copy-start(f32[4,4,1440]{2,0,1:T(4,128)S(1)} %copy.8) | copy-start | bytes 276484
  53.6 9.1 %copy-start.4 = (f32[4,4,1440]{2,0,1:T(4,128)}, f32[4,4,1440]{2,0,1:T(4,128)S(1)}, u32[]{:S(2)}) copy-start(f32[4,4,1440]{2,0,1:T(4,128)S(1)} %copy.9) | copy-start | bytes 276484
  74.4 7.6 %copy-start.8 = (s32[4,1440]{1,0:T(4,128)S(1)}, s32[4,1440]{1,0:T(4,128)}, u32[]{:S(2)}) copy-start(s32[4,1440]{1,0:T(4,128)} %param.6) | copy-start | bytes 69124
  76.2 18.5 %collective-permute-start.4 = (f32[30,4,2,1440]{3,1,2,0:T(4,128)}, f32[30,4,2,1440]{3,1,2,0:T(4,128)}, u32[]{:S(2)}, u32[]{:S(2)}) collective-permute-start(f32[30,4,2,1440]{3,1,2,0:T(4,128)} %get-tuple-element.18), channel_id=1, source_target_pairs={{0,1},{1,2},{2,3},{3,4},{4,5},{5,6},{6,7},{7,8},{8,9},{9,10},{10,1... | collective-permute-start | bytes 4147208 | tf_op jit(solution)/shard_map/ppermute | solution.py:12
  78.2 21.0 %collective-permute-start.5 = (f32[30,4,2,1440]{3,1,2,0:T(4,128)}, f32[30,4,2,1440]{3,1,2,0:T(4,128)}, u32[]{:S(2)}, u32[]{:S(2)}) collective-permute-start(f32[30,4,2,1440]{3,1,2,0:T(4,128)} %get-tuple-element.17), channel_id=1, source_target_pairs={{1,0},{2,1},{3,2},{4,3},{5,4},{6,5},{7,6},{8,7},{9,8},{10,9},{11,1... | collective-permute-start | bytes 4147208 | tf_op jit(solution)/shard_map/ppermute | solution.py:15
  106.4 3.9 %copy-start.3 = (f32[4,4,1440]{2,0,1:T(4,128)S(1)}, f32[4,4,1440]{2,0,1:T(4,128)}, u32[]{:S(2)}) copy-start(f32[4,4,1440]{2,0,1:T(4,128)} %copy-done.2) | copy-start | bytes 276484
  106.4 3.9 %copy-start.5 = (f32[4,4,1440]{2,0,1:T(4,128)S(1)}, f32[4,4,1440]{2,0,1:T(4,128)}, u32[]{:S(2)}) copy-start(f32[4,4,1440]{2,0,1:T(4,128)} %copy-done.4) | copy-start | bytes 276484
  110.3 5.0 %copy-start = (f32[30,4,4,1440]{3,2,1,0:T(4,128)S(1)}, f32[30,4,4,1440]{3,2,1,0:T(4,128)}, u32[]{:S(2)}) copy-start(f32[30,4,4,1440]{3,2,1,0:T(4,128)} %param.4) | copy-start | bytes 8294404
  110.3 5.0 %copy-start.7 = (f32[4,4,1440]{2,0,1:T(4,128)S(1)}, f32[4,4,1440]{2,0,1:T(4,128)}, u32[]{:S(2)}) copy-start(f32[4,4,1440]{2,0,1:T(4,128)} %copy.13) | copy-start | bytes 276484
where the time goes:
time: 124 us; the launch traced here: 123 us
  other arithmetic  39.6 us (32%)
  local copies, waits for them, and re-layouts  39.2 us (32%)
  starting transfers between devices  35.7 us (29%)
  waiting for transfers between devices  7.68 us (6%)
    ppermute x3, starting transfers between devices, extended(): lax.ppermute(lax.slice_in_dim(block, 0, width, axis=dim), axis, backward)  27.2 us
    unnamed x25, local copies, waits for them, and re-layouts  23.6 us
    mul x2, other arithmetic, advect_section(): east_open * face_flux(east_face, jnp.roll(field, 1, -1), field, jnp.roll(...  9.57 us
    ppermute x3, starting transfers between devices, extended(): lax.ppermute(lax.slice_in_dim(block, block.shape[dim] - width, None, axis...  8.47 us
    select_n x3, other arithmetic, north_fold(): return jnp.where(is_top, folded, padded)  8.23 us
    mul x2, other arithmetic, advect_section(): north_open * face_flux(north_face, padded[..., 0:rows + 1, :], padded[......  7.69 us
    ppermute x3, waiting for transfers between devices, extended(): lax.ppermute(lax.slice_in_dim(block, 0, width, axis=dim), axis, backward)  5.92 us
    mul x2, other arithmetic, shards(): return 0.5 * (start + second) * wet  4.53 us
  transfers between devices with their start and end apart: 6, of which 3 were waited for; matrix products, arithmetic and copies ran while one was open for 26% of the time, Pallas kernels for 0%

commit v1 on v0

v1 whole, which is shorter than its diff:
```python
import functools

import jax
import jax.numpy as jnp
from jax import lax
from jax.experimental import pallas as pl
from jax.experimental.pallas import tpu as pltpu
from jax.sharding import PartitionSpec as P


LANES = 128
SMALL = 24
CHUNKS = (8, 16, 6)


def lane_index():
    return lax.broadcasted_iota(jnp.int32, (8, LANES), 1)


def spread(ref, row):
    return jnp.broadcast_to(ref[pl.ds(row, 1), :], (8, LANES))


def wrap_tile(raw, first, rem):
    lane = lane_index()
    wrapped = jnp.where(
        lane < LANES - rem, pltpu.roll(first, rem, 1), pltpu.roll(raw, LANES - rem, 1)
    )
    return jnp.where(lane < rem, raw, wrapped)


def shifted(tiles, t, by):
    lane = lane_index()
    count = len(tiles)
    if by > 0:
        here, there = tiles[t], tiles[(t + 1) % count]
        keep = lane < LANES - by
    else:
        here, there = tiles[t], tiles[(t - 1) % count]
        keep = lane >= -by
    amount = (-by) % LANES
    return jnp.where(keep, pltpu.roll(here, amount, 1), pltpu.roll(there, amount, 1))


def mirrored(tiles, rem):
    lane = lane_index()
    index = (rem - 1 - lane) % LANES
    turned = [jnp.take_along_axis(tile, index, axis=1, mode="promise_in_bounds") for tile in tiles]
    last = len(tiles) - 1
    out = [jnp.where(lane < rem, turned[last - t], turned[last - 1 - t]) for t in range(last)]
    out.append(wrap_tile(turned[0], out[0], rem))
    return out


def natural_tile(ref, where, t, lon):
    full, rem = divmod(lon, LANES)
    if t < full:
        return ref[(*where, slice(None), pl.ds(t * LANES, LANES))]
    tail = ref[(*where, slice(None), pl.ds(full * LANES, rem))]
    head = ref[(*where, slice(None), pl.ds(0, LANES))][:, : LANES - 2 * rem]
    return jnp.concatenate([tail, head, tail], axis=1)


def stage_currents(currents, levels, held, lon):
    tiles = lon // LANES + 1
    for t in range(tiles):
        for c in range(2):
            for half in range(2):
                pair = [natural_tile(currents, (c, 2 * half + k), t, lon) for k in range(2)]
                held[pl.ds((t * 5 + 2 * c + half) * 8, 8), :] = jnp.concatenate(pair, axis=0)
        column = natural_tile(levels, (), t, lon).astype(jnp.float32)
        held[pl.ds((t * 5 + 4) * 8, 8), :] = jnp.concatenate([column, column], axis=0)


def own_row(held, t, c, row):
    return held[pl.ds((t * 5 + 2 * c) * 8 + row, 4, stride=4), :]


def edge_rows(held, out, base, north, lon):
    u0, v0 = jnp.where(north, 2, 0), jnp.where(north, 1, 0)
    for t in range(lon // LANES + 1):
        u = [own_row(held, t, 0, u0 + k) for k in range(2)]
        v = [own_row(held, t, 1, v0 + k) for k in range(3)]
        column = held[pl.ds((t * 5 + 4) * 8, 4), :]
        start = base + t * SMALL
        out[pl.ds(start, 8), :] = jnp.concatenate(u, axis=0)
        out[pl.ds(start + 8, 8), :] = jnp.concatenate(v[:2], axis=0)
        out[pl.ds(start + 16, 8), :] = jnp.concatenate([v[2], column], axis=0)


def pack_kernel(offset, n, lon, small, *refs):
    if small:
        x_hbm, currents, levels, out, near_small, x, held, sem = refs
    else:
        x_hbm, out, x, sem = refs
    full, rem = divmod(lon, LANES)
    copy = pltpu.make_async_copy(x_hbm.at[pl.ds(offset, n)], x, sem)
    copy.start()
    if small:
        odd = lax.axis_index("lat") % 2 == 1
        stage_currents(currents, levels, held, lon)
        edge_rows(held, out, (16 * full + 4) * n, odd, lon)
        edge_rows(held, near_small, 0, jnp.logical_not(odd), lon)
    copy.wait()

    def pair(g, carry):
        tails = []
        for k in range(2):
            for half in range(2):
                for t in range(full):
                    rows = [x[2 * g + k, 2 * half + s, :, pl.ds(t * LANES, LANES)] for s in range(2)]
                    start = pl.multiple_of((t * n + 2 * g + k) * 16 + 8 * half, 8)
                    out[pl.ds(start, 8), :] = jnp.concatenate(rows, axis=0)
            tail = [x[2 * g + k, level, :, pl.ds(full * LANES, rem)] for level in range(4)]
            tails.append(jnp.concatenate(tail, axis=1))
        start = pl.multiple_of(16 * full * n + 8 * g, 8)
        out[pl.ds(start, 8), :] = jnp.concatenate(tails, axis=0)
        return carry

    lax.fori_loop(0, n // 2, pair, 0)


def coefficient_kernel(n, lon, currents, levels, near, far, k1, k2, held, u, v, w):
    full, rem = divmod(lon, LANES)
    tiles = full + 1
    far_base = (16 * full + 4) * n
    place = lax.axis_index("lat")
    odd = place % 2 == 1
    level = (lax.broadcasted_iota(jnp.int32, (8, LANES), 0) % 4).astype(jnp.float32)
    stage_currents(currents, levels, held, lon)

    def put(dst, row, t, value):
        dst[pl.ds((row * tiles + t) * 8, 8), :] = value

    def get(src, row):
        return [src[pl.ds((row * tiles + t) * 8, 8), :] for t in range(tiles)]

    def twice(value):
        return jnp.concatenate([value, value], axis=0)

    for t in range(tiles):
        for row in range(4):
            put(u, 2 + row, t, twice(own_row(held, t, 0, row)))
            put(v, 3 + row, t, twice(own_row(held, t, 1, row)))
            column = spread(held, (t * 5 + 4) * 8 + row)
            put(w, 4 + row, t, (level < column).astype(jnp.float32))
        sides = ((0, 0, 0, True), (6, 7, 8, False))
        for u_row, v_row, w_row, is_low in sides:
            take_near = odd if is_low else jnp.logical_not(odd)

            def pick(start, size):
                a = near[pl.ds(t * SMALL + start, size), :]
                b = far[pl.ds(far_base + t * SMALL + start, size), :]
                return jnp.where(take_near, a, b)

            for k in range(2):
                put(u, u_row + k, t, twice(pick(4 * k, 4)))
            for k in range(3):
                put(v, v_row + k, t, twice(pick(8 + 4 * k, 4)))
            for k in range(4):
                put(w, w_row + k, t, (level < jnp.broadcast_to(pick(20 + k, 1), level.shape)).astype(jnp.float32))

    @pl.when(place == lax.axis_size("lat") - 1)
    def _():
        for dst, first, count, sign in ((u, 6, 2, -1.0), (v, 7, 3, -1.0), (w, 8, 4, 1.0)):
            for k in range(count):
                for t, value in enumerate(mirrored(get(dst, first - 1 - k), rem)):
                    put(dst, first + k, t, sign * value)

    def parts(face):
        return jnp.maximum(face, 0.0) * (1.0 / 6.0), jnp.minimum(face, 0.0) * (1.0 / 6.0)

    def north_faces(row):
        wa, wb, va, vb = get(w, row + 4), get(w, row + 5), get(v, row + 3), get(v, row + 4)
        return [parts(wa[t] * wb[t] * (0.5 * (va[t] + vb[t]))) for t in range(tiles)]

    south = north_faces(-3)
    for row in range(-2, 6):
        north = north_faces(row)
        ur = get(u, row + 2)
        wr = {d: get(w, row + 4 + d) for d in (-2, -1, 0, 1, 2)}
        we = {d: [shifted(wr[0], t, d) for t in range(tiles)] for d in (-2, -1, 1, 2)}
        east = [parts(wr[0][t] * we[1][t] * (0.5 * (ur[t] + shifted(ur, t, 1)))) for t in range(tiles)]
        west_p = [shifted([e[0] for e in east], t, -1) for t in range(tiles)]
        west_m = [shifted([e[1] for e in east], t, -1) for t in range(tiles)]
        for t in range(tiles):
            (p, m), (q, s), (qs, ss) = east[t], north[t], south[t]
            pw, mw = west_p[t], west_m[t]
            plain = [
                -pw,
                p + 5.0 * pw + 2.0 * mw,
                -(2.0 * p + 5.0 * m + mw),
                m,
                1.0 - (5.0 * p + 2.0 * m) + (2.0 * pw + 5.0 * mw) - (5.0 * q + 2.0 * s) + (2.0 * qs + 5.0 * ss),
                -qs,
                q + 5.0 * qs + 2.0 * ss,
                -(2.0 * q + 5.0 * s + ss),
                s,
            ]
            source = [we[-2][t], we[-1][t], we[1][t], we[2][t], wr[0][t], wr[-2][t], wr[-1][t], wr[1][t], wr[2][t]]
            here = wr[0][t]
            for k in range(9):
                k1[pl.ds((((row + 2) * tiles + t) * 9 + k) * 8, 8), :] = plain[k] * source[k] * here
            if 0 <= row < 4:
                half = 0.5 * here
                for k in range(9):
                    k2[pl.ds(((row * tiles + t) * 10 + k) * 8, 8), :] = plain[k] * half
                k2[pl.ds(((row * tiles + t) * 10 + 9) * 8, 8), :] = half * here
        south = north


def stencil(coefficient, lon_row, rows, t):
    values = [shifted(lon_row, t, d) for d in (-2, -1, 1, 2)] + [lon_row[t]] + rows
    total = coefficient(0) * values[0]
    for k in range(1, 9):
        total = total + coefficient(k) * values[k]
    return total


def advect_kernel(n, lon, own, near, far, k1, k2, *refs):
    out, f, first, turned = refs[-4:]
    full, rem = divmod(lon, LANES)
    tiles = full + 1
    row_size = tiles * 8
    g = pl.program_id(0)
    place = lax.axis_index("lat")
    odd = place % 2 == 1
    sub = lax.broadcasted_iota(jnp.int32, (8, LANES), 0)

    near_base = jnp.where(odd, 0, 8) * row_size
    far_base = jnp.where(odd, 8, 0) * row_size
    for source, base in ((near, near_base), (own, 4 * row_size), (far, far_base)):
        for r in range(4):
            for t in range(full):
                value = source[pl.ds((t * n + 2 * g) * 16 + r, 8, stride=4), :]
                f[pl.ds(pl.multiple_of(base + (r * tiles + t) * 8, 8), 8), :] = value
                if t == 0:
                    start = value
            tail = 16 * full * n + 8 * g
            a = spread(source, tail + r)
            b = spread(source, tail + 4 + r)
            both = jnp.where(sub < 4, a, b)
            raw = both
            for level in range(1, 4):
                raw = jnp.where(sub % 4 == level, pltpu.roll(both, LANES - rem * level, 1), raw)
            f[pl.ds(pl.multiple_of(base + (r * tiles + full) * 8, 8), 8), :] = wrap_tile(raw, start, rem)

    def row_of(ref, row):
        return [ref[pl.ds((row * tiles + t) * 8, 8), :] for t in range(tiles)]

    @pl.when(place == lax.axis_size("lat") - 1)
    def _():
        for k in range(4):
            for t, value in enumerate(mirrored(row_of(f, 7 - k), rem)):
                f[pl.ds(((8 + k) * tiles + t) * 8, 8), :] = value

    for row in range(8):
        lon_row = row_of(f, row + 2)
        for t in range(tiles):
            rows = [f[pl.ds(((row + 2 + d) * tiles + t) * 8, 8), :] for d in (-2, -1, 1, 2)]
            base = (row * tiles + t) * 9
            value = stencil(lambda k: k1[pl.ds((base + k) * 8, 8), :], lon_row, rows, t)
            first[pl.ds((row * tiles + t) * 8, 8), :] = value

    for row in range(4):
        lon_row = row_of(first, row + 2)
        for t in range(tiles):
            rows = [first[pl.ds(((row + 2 + d) * tiles + t) * 8, 8), :] for d in (-2, -1, 1, 2)]
            base = (row * tiles + t) * 10
            value = stencil(lambda k: k2[pl.ds((base + k) * 8, 8), :], lon_row, rows, t)
            value = value + k2[pl.ds((base + 9) * 8, 8), :] * f[pl.ds(((row + 4) * tiles + t) * 8, 8), :]
            turned[pl.ds(t * 32 + row, 8, stride=4), :] = value

    for k in range(2):
        for level in range(4):
            for t in range(tiles):
                value = turned[pl.ds(t * 32 + (4 * k + level) * 4, 4), :]
                if t < full:
                    out[k, level, :, pl.ds(t * LANES, LANES)] = value
                else:
                    out[k, level, :, pl.ds(full * LANES, rem)] = value[:, :rem]


def vmem():
    return pl.BlockSpec(memory_space=pltpu.VMEM)


def shards(tracers, currents, column_levels):
    count = lax.axis_size("lat")
    total, levels, rows, lon = tracers.shape
    full, rem = divmod(lon, LANES)
    tiles = full + 1
    assert levels == 4 and rows == 4 and 4 * rem == LANES and count % 2 == 0 and sum(CHUNKS) == total
    near_pairs = [(i, i ^ 1) for i in range(count)]
    far_pairs = [pair for i in range(1, count - 1, 2) for pair in ((i, i + 1), (i + 1, i))]
    f32 = jnp.float32
    offsets = [sum(CHUNKS[:i]) for i in range(len(CHUNKS))]

    packed, near_small = [], None
    for i, (offset, n) in enumerate(zip(offsets, CHUNKS)):
        small = i == 0
        size = (16 * full + 4) * n
        shape = [jax.ShapeDtypeStruct((size + (SMALL * tiles if small else 0), LANES), f32)]
        scratch = [pltpu.VMEM((n, levels, rows, lon), f32), pltpu.SemaphoreType.DMA]
        if small:
            shape.append(jax.ShapeDtypeStruct((SMALL * tiles, LANES), f32))
            scratch.insert(1, pltpu.VMEM((tiles * 40, LANES), f32))
        result = pl.pallas_call(
            functools.partial(pack_kernel, offset, n, lon, small),
            out_shape=shape,
            in_specs=[pl.BlockSpec(memory_space=pl.ANY)] + [vmem()] * (2 if small else 0),
            out_specs=[vmem() for _ in shape],
            scratch_shapes=scratch,
            cost_estimate=pl.CostEstimate(flops=1000000 * n, bytes_accessed=n * 184320, transcendentals=0),
            compiler_params=pltpu.CompilerParams(vmem_limit_bytes=16 * 2**20),
        )(tracers, *((currents, column_levels) if small else ()))
        packed.append(result[0])
        if small:
            near_small = result[1]
    far = []
    for i in range(len(CHUNKS)):
        far.append(lax.ppermute(packed[i], "lat", far_pairs))
    small_received = lax.ppermute(near_small, "lat", near_pairs)
    near = []
    for i in range(len(CHUNKS)):
        near.append(lax.ppermute(packed[i], "lat", near_pairs))
    k1, k2 = pl.pallas_call(
        functools.partial(coefficient_kernel, CHUNKS[0], lon),
        out_shape=[
            jax.ShapeDtypeStruct((8 * tiles * 9 * 8, LANES), f32),
            jax.ShapeDtypeStruct((4 * tiles * 10 * 8, LANES), f32),
        ],
        in_specs=[vmem()] * 4,
        out_specs=[vmem()] * 2,
        scratch_shapes=[
            pltpu.VMEM((tiles * 40, LANES), f32),
            pltpu.VMEM((8 * tiles * 8, LANES), f32),
            pltpu.VMEM((10 * tiles * 8, LANES), f32),
            pltpu.VMEM((12 * tiles * 8, LANES), f32),
        ],
        cost_estimate=pl.CostEstimate(flops=8000000, bytes_accessed=6000000, transcendentals=0),
        compiler_params=pltpu.CompilerParams(vmem_limit_bytes=20 * 2**20),
        name="coefficients",
    )(currents, column_levels, small_received, far[0])
    out = None
    for i, (offset, n) in enumerate(zip(offsets, CHUNKS)):
        operands = [packed[i], near[i], far[i], k1, k2]
        specs = [vmem()] * 5
        aliases = {}
        if out is not None:
            aliases = {len(operands): 0}
            operands.append(out)
            specs.append(pl.BlockSpec(memory_space=pl.ANY))
        out = pl.pallas_call(
            functools.partial(advect_kernel, n, lon),
            out_shape=jax.ShapeDtypeStruct(tracers.shape, f32),
            grid=(n // 2,),
            in_specs=specs,
            out_specs=pl.BlockSpec((2, levels, rows, lon), lambda g, o=offset // 2: (o + g, 0, 0, 0)),
            scratch_shapes=[
                pltpu.VMEM((12 * tiles * 8, LANES), f32),
                pltpu.VMEM((8 * tiles * 8, LANES), f32),
                pltpu.VMEM((32 * tiles, LANES), f32),
            ],
            input_output_aliases=aliases,
            cost_estimate=pl.CostEstimate(flops=3000000 * n, bytes_accessed=n * 500000, transcendentals=0),
            compiler_params=pltpu.CompilerParams(vmem_limit_bytes=24 * 2**20),
        )(*operands)
    return out


def solution(mesh):
    in_specs = (
        P("member", None, "lat", None),
        P("member", None, "lat", None),
        P(("member", "lat"), None),
    )
    out_specs = P("member", None, "lat", None)
    return jax.shard_map(shards, mesh=mesh, in_specs=in_specs, out_specs=out_specs, check_vma=False)
```

time: 124 us -> 75 us (0.60)
  other arithmetic: 39.6 us -> 0 us
  local copies, waits for them, and re-layouts: 39.2 us -> 1.84 us
  Pallas kernels: 0 us -> 21.1 us
  waiting for transfers between devices: 7.68 us -> 22.9 us
  starting transfers between devices: 35.7 us -> 28.8 us
    mul x11 -> x0, other arithmetic: 28 us -> none  [the longest x2 9.57 us: advect_section(): east_open * face_flux(east_face, jnp.roll(field, 1, -1), field, jnp.roll(...]
    unnamed x25 -> x6, local copies, waits for them, and re-layouts: 23.6 us -> 1.84 us
    pallas_call x0 -> x7, Pallas kernels: none -> 21.1 us  [the longest x3 17.9 us: shards(): pl.pallas_call(functools.partial(advect_kernel, n, lon), out_shape=jax.Sh...]
    ppermute x6 -> x7, waiting for transfers between devices: 7.68 us -> 22.9 us  [the longest x3 21.2 us: shards(): far.append(lax.ppermute(packed[i], 'lat', far_pairs))]
    slice x16 -> x0, local copies, waits for them, and re-layouts: 11.7 us -> none  [the longest x4 4.16 us: advect_section(): jnp.roll(field, -1, -1)]
    select_n x3 -> x0, other arithmetic: 8.23 us -> none  [north_fold(): return jnp.where(is_top, folded, padded)]
    ppermute x6 -> x7, starting transfers between devices: 35.7 us -> 28.8 us  [the longest x3 20.8 us: shards(): near.append(lax.ppermute(packed[i], 'lat', near_pairs))]
    mul x6 -> x0, local copies, waits for them, and re-layouts: 3.66 us -> none  [the longest x2 3.41 us: shards(): return 0.5 * (start + second) * wet]
  transfers between devices with their start and end apart: 6 -> 7, of which waited for: 3 -> 2; matrix products, arithmetic and copies ran while one was open for 26% -> 0% of each run, Pallas kernels for 0% -> 22%
where the time goes in v1:
time: 75 us; the launch traced here: 74.8 us
  starting transfers between devices  28.8 us (38%)
  waiting for transfers between devices  22.9 us (31%)
  Pallas kernels  21.1 us (28%)
  local copies, waits for them, and re-layouts  1.84 us (2%)
    ppermute x3, waiting for transfers between devices, shards(): far.append(lax.ppermute(packed[i], 'lat', far_pairs))  21.2 us
    ppermute x3, starting transfers between devices, shards(): near.append(lax.ppermute(packed[i], 'lat', near_pairs))  20.8 us
    pallas_call x3, Pallas kernels, shards(): pl.pallas_call(functools.partial(advect_kernel, n, lon), out_shape=jax.Sh...  17.9 us
    ppermute x3, starting transfers between devices, shards(): far.append(lax.ppermute(packed[i], 'lat', far_pairs))  7.55 us
    unnamed x6, local copies, waits for them, and re-layouts  1.84 us
    ppermute x1, waiting for transfers between devices, shards(): small_received = lax.ppermute(near_small, 'lat', near_pairs)  1.77 us
    pallas_call x1, Pallas kernels, shards(): pl.pallas_call(functools.partial(coefficient_kernel, CHUNKS[0], lon), out...  1.65 us
    pallas_call x3, Pallas kernels, shards(): pl.pallas_call(functools.partial(pack_kernel, offset, n, lon, small), out...  1.53 us
  transfers between devices with their start and end apart: 7, of which 2 were waited for; matrix products, arithmetic and copies ran while one was open for 0% of the time, Pallas kernels for 22%

profile of v1, /device:TPU:33, one launch (start us, length us, event | category | flops | bytes accessed | tf_op | source)
XLA Modules:
  0.0 74.8 jit_solution(3159014727911760046)
XLA Ops:
  0.0 0.0 copy-start
  0.0 1.8 %copy-done = f32[30,4,4,1440]{3,2,1,0:T(4,128)S(1)} copy-done((f32[30,4,4,1440]{3,2,1,0:T(4,128)S(1)}, f32[30,4,4,1440]{3,2,1,0:T(4,128)}, u32[]{:S(2)}) %copy-start) | copy-done | bytes 2764824
  1.8 0.0 copy-start.1
  1.8 0.0 copy-start.2
  1.8 0.7 shard_map.39.own
  2.6 20.5 %collective-permute-start.4 = (f32[2880,128]{1,0:T(8,128)S(1)}, f32[2880,128]{1,0:T(8,128)S(1)}, u32[]{:S(2)}, u32[]{:S(2)}) collective-permute-start(f32[2880,128]{1,0:T(8,128)S(1)} %shard_map.39.own), channel_id=1, source_target_pairs={{0,1},{1,0},{2,3},{3,2},{4,5},{5,4},{6,7},{7,6},{8,9},{9,8},{10,11... | collective-permute-start | bytes 4423688 | tf_op jit(solution)/shard_map/ppermute | solution.py:326
  23.1 1.9 %collective-permute-start.5 = (f32[2880,128]{1,0:T(8,128)S(1)}, f32[2880,128]{1,0:T(8,128)S(1)}, u32[]{:S(2)}, u32[]{:S(2)}) collective-permute-start(f32[2880,128]{1,0:T(8,128)S(1)} %shard_map.39.own), channel_id=1, source_target_pairs={{1,2},{2,1},{3,4},{4,3},{5,6},{6,5},{7,8},{8,7},{9,10},{10,9},{11,... | collective-permute-start | bytes 4423688 | tf_op jit(solution)/shard_map/ppermute | solution.py:322
  25.0 0.0 copy-done.1
  25.1 0.0 copy-done.2
  25.1 0.5 shard_map.38
  25.5 3.7 %collective-permute-start.3 = (f32[1728,128]{1,0:T(8,128)S(1)}, f32[1728,128]{1,0:T(8,128)S(1)}, u32[]{:S(2)}, u32[]{:S(2)}) collective-permute-start(f32[1728,128]{1,0:T(8,128)S(1)} %get-tuple-element.10.own), channel_id=1, source_target_pairs={{1,2},{2,1},{3,4},{4,3},{5,6},{6,5},{7,8},{8,7},{9,10},{10,9},{11,... | collective-permute-start | bytes 2654216 | tf_op jit(solution)/shard_map/ppermute | solution.py:322
  29.2 0.1 collective-permute-start.6
  29.4 0.5 collective-permute-start.2
  29.9 0.3 shard_map.37.own
  30.2 1.8 %collective-permute-done.2.near = f32[288,128]{1,0:T(8,128)S(1)} collective-permute-done((f32[288,128]{1,0:T(8,128)S(1)}, f32[288,128]{1,0:T(8,128)S(1)}, u32[]{:S(2)}, u32[]{:S(2)}) %collective-permute-start.2) | collective-permute-done | bytes 147488 | tf_op jit(solution)/shard_map/ppermute | solution.py:323
  32.0 0.1 collective-permute-start
  32.1 21.2 %collective-permute-done.3.far = f32[1728,128]{1,0:T(8,128)S(1)} collective-permute-done((f32[1728,128]{1,0:T(8,128)S(1)}, f32[1728,128]{1,0:T(8,128)S(1)}, u32[]{:S(2)}, u32[]{:S(2)}) %collective-permute-start.3) | collective-permute-done | bytes 884768 | tf_op jit(solution)/shard_map/ppermute | solution.py:322
  53.3 1.9 %collective-permute-start.1 = (f32[1080,128]{1,0:T(8,128)S(1)}, f32[1080,128]{1,0:T(8,128)S(1)}, u32[]{:S(2)}, u32[]{:S(2)}) collective-permute-start(f32[1080,128]{1,0:T(8,128)S(1)} %shard_map.37.own), channel_id=1, source_target_pairs={{1,2},{2,1},{3,4},{4,3},{5,6},{6,5},{7,8},{8,7},{9,10},{10,9},{11,... | collective-permute-start | bytes 1658888 | tf_op jit(solution)/shard_map/ppermute | solution.py:322
  55.2 1.7 %coefficients.1 = (f32[6912,128]{1,0:T(8,128)S(1)}, f32[3840,128]{1,0:T(8,128)S(1)}) custom-call(f32[2,4,4,1440]{3,2,1,0:T(4,128)S(1)} %copy-done.1, s32[4,1440]{1,0:T(4,128)S(1)} %copy-done.2, f32[288,128]{1,0:T(8,128)S(1)} %collective-permute-done.2.near, f32[1728,128]{1,0:T(8,128)S(1)} %collective-permute-done.3.far), custom_call_target="tpu_custom_call" | custom-call | flops 8000000 | bytes 6000000 | tf_op jit(solution)/shard_map/coefficients/pallas_call | solution.py:327
  56.9 0.0 collective-permute-done.6.near
  56.9 4.9 %shard_map.40.refs_0_ = f32[30,4,4,1440]{3,2,1,0:T(4,128)} custom-call(f32[1728,128]{1,0:T(8,128)S(1)} %get-tuple-element.10.own, f32[1728,128]{1,0:T(8,128)S(1)} %collective-permute-done.6.near, f32[1728,128]{1,0:T(8,128)S(1)} %collective-permute-done.3.far, f32[6912,128]{1,0:T(8,128)S(1)} %get-tuple-element.11.k1, f32[3840,128]{1,0:T(8,128)S(1)} %get-tuple-element.12.k2), custom_call_target="tpu_custom_call" | custom-call | flops 24000000 | bytes 4000000 | tf_op jit(solution)/shard_map/pallas_call | solution.py:354
  61.8 0.0 collective-permute-done.4.near
  61.8 0.0 collective-permute-done.5.far
  61.8 9.1 %shard_map.41.refs_0_ = f32[30,4,4,1440]{3,2,1,0:T(4,128)} custom-call(f32[2880,128]{1,0:T(8,128)S(1)} %shard_map.39.own, f32[2880,128]{1,0:T(8,128)S(1)} %collective-permute-done.4.near, f32[2880,128]{1,0:T(8,128)S(1)} %collective-permute-done.5.far, f32[6912,128]{1,0:T(8,128)S(1)} %get-tuple-element.11.k1, ...), custom_call_target="tpu_custom_call", output_to_operand_aliasing={{}: (5, {})} | custom-call | flops 48000000 | bytes 8000000 | tf_op jit(solution)/shard_map/pallas_call | solution.py:354
  70.9 0.0 collective-permute-done.near
  70.9 0.0 collective-permute-done.1.far
  70.9 3.9 %shard_map.42 = f32[30,4,4,1440]{3,2,1,0:T(4,128)} custom-call(f32[1080,128]{1,0:T(8,128)S(1)} %shard_map.37.own, f32[1080,128]{1,0:T(8,128)S(1)} %collective-permute-done.near, f32[1080,128]{1,0:T(8,128)S(1)} %collective-permute-done.1.far, f32[6912,128]{1,0:T(8,128)S(1)} %get-tuple-element.11.k1, ...), custom_call_target="tpu_custom_call", output_to_operand_aliasing={{}: (5, {})} | custom-call | flops 18000000 | bytes 3000000 | tf_op jit(solution)/shard_map/pallas_call | solution.py:354
Async XLA Ops:
  0.0 1.8 %copy-start = (f32[30,4,4,1440]{3,2,1,0:T(4,128)S(1)}, f32[30,4,4,1440]{3,2,1,0:T(4,128)}, u32[]{:S(2)}) copy-start(f32[30,4,4,1440]{3,2,1,0:T(4,128)} %refs_0_.5) | copy-start | bytes 8294404
  1.8 23.2 %copy-start.1 = (f32[2,4,4,1440]{3,2,1,0:T(4,128)S(1)}, f32[2,4,4,1440]{3,2,1,0:T(4,128)}, u32[]{:S(2)}) copy-start(f32[2,4,4,1440]{3,2,1,0:T(4,128)} %currents.1) | copy-start | bytes 552964
  1.8 23.2 %copy-start.2 = (s32[4,1440]{1,0:T(4,128)S(1)}, s32[4,1440]{1,0:T(4,128)}, u32[]{:S(2)}) copy-start(s32[4,1440]{1,0:T(4,128)} %levels.1) | copy-start | bytes 69124
  2.6 59.2 %collective-permute-start.4 = (f32[2880,128]{1,0:T(8,128)S(1)}, f32[2880,128]{1,0:T(8,128)S(1)}, u32[]{:S(2)}, u32[]{:S(2)}) collective-permute-start(f32[2880,128]{1,0:T(8,128)S(1)} %shard_map.39.own), channel_id=1, source_target_pairs={{0,1},{1,0},{2,3},{3,2},{4,5},{5,4},{6,7},{7,6},{8,9},{9,8},{10,11... | collective-permute-start | bytes 4423688 | tf_op jit(solution)/shard_map/ppermute | solution.py:326
  23.1 38.7 %collective-permute-start.5 = (f32[2880,128]{1,0:T(8,128)S(1)}, f32[2880,128]{1,0:T(8,128)S(1)}, u32[]{:S(2)}, u32[]{:S(2)}) collective-permute-start(f32[2880,128]{1,0:T(8,128)S(1)} %shard_map.39.own), channel_id=1, source_target_pairs={{1,2},{2,1},{3,4},{4,3},{5,6},{6,5},{7,8},{8,7},{9,10},{10,9},{11,... | collective-permute-start | bytes 4423688 | tf_op jit(solution)/shard_map/ppermute | solution.py:322
  25.5 27.7 %collective-permute-start.3 = (f32[1728,128]{1,0:T(8,128)S(1)}, f32[1728,128]{1,0:T(8,128)S(1)}, u32[]{:S(2)}, u32[]{:S(2)}) collective-permute-start(f32[1728,128]{1,0:T(8,128)S(1)} %get-tuple-element.10.own), channel_id=1, source_target_pairs={{1,2},{2,1},{3,4},{4,3},{5,6},{6,5},{7,8},{8,7},{9,10},{10,9},{11,... | collective-permute-start | bytes 2654216 | tf_op jit(solution)/shard_map/ppermute | solution.py:322
  29.2 27.7 %collective-permute-start.6 = (f32[1728,128]{1,0:T(8,128)S(1)}, f32[1728,128]{1,0:T(8,128)S(1)}, u32[]{:S(2)}, u32[]{:S(2)}) collective-permute-start(f32[1728,128]{1,0:T(8,128)S(1)} %get-tuple-element.10.own), channel_id=1, source_target_pairs={{0,1},{1,0},{2,3},{3,2},{4,5},{5,4},{6,7},{7,6},{8,9},{9,8},{10,11... | collective-permute-start | bytes 2654216 | tf_op jit(solution)/shard_map/ppermute | solution.py:326
  29.4 2.6 %collective-permute-start.2 = (f32[288,128]{1,0:T(8,128)S(1)}, f32[288,128]{1,0:T(8,128)S(1)}, u32[]{:S(2)}, u32[]{:S(2)}) collective-permute-start(f32[288,128]{1,0:T(8,128)S(1)} %get-tuple-element.9), channel_id=1, source_target_pairs={{0,1},{1,0},{2,3},{3,2},{4,5},{5,4},{6,7},{7,6},{8,9},{9,8},{10,11... | collective-permute-start | bytes 442376 | tf_op jit(solution)/shard_map/ppermute | solution.py:323
  32.0 39.0 %collective-permute-start = (f32[1080,128]{1,0:T(8,128)S(1)}, f32[1080,128]{1,0:T(8,128)S(1)}, u32[]{:S(2)}, u32[]{:S(2)}) collective-permute-start(f32[1080,128]{1,0:T(8,128)S(1)} %shard_map.37.own), channel_id=1, source_target_pairs={{0,1},{1,0},{2,3},{3,2},{4,5},{5,4},{6,7},{7,6},{8,9},{9,8},{10,11... | collective-permute-start | bytes 1658888 | tf_op jit(solution)/shard_map/ppermute | solution.py:326
  53.3 17.7 %collective-permute-start.1 = (f32[1080,128]{1,0:T(8,128)S(1)}, f32[1080,128]{1,0:T(8,128)S(1)}, u32[]{:S(2)}, u32[]{:S(2)}) collective-permute-start(f32[1080,128]{1,0:T(8,128)S(1)} %shard_map.37.own), channel_id=1, source_target_pairs={{1,2},{2,1},{3,4},{4,3},{5,6},{6,5},{7,8},{8,7},{9,10},{10,9},{11,... | collective-permute-start | bytes 1658888 | tf_op jit(solution)/shard_map/ppermute | solution.py:322

commit v2 on v1

v2 whole, which is shorter than its diff:
```python
import functools

import jax
import jax.numpy as jnp
from jax import lax
from jax.experimental import pallas as pl
from jax.experimental.pallas import tpu as pltpu
from jax.sharding import PartitionSpec as P


LANES = 128
SMALL = 24
CHUNKS = (12, 8, 6, 4)
OFFSETS = (0, 12, 24, 20)
GROUPS = (3, 2, 3, 2)


def lane_index():
    return lax.broadcasted_iota(jnp.int32, (8, LANES), 1)


def spread(ref, row):
    return jnp.broadcast_to(ref[pl.ds(row, 1), :], (8, LANES))


def wrap_tile(raw, first, rem):
    lane = lane_index()
    wrapped = jnp.where(
        lane < LANES - rem, pltpu.roll(first, rem, 1), pltpu.roll(raw, LANES - rem, 1)
    )
    return jnp.where(lane < rem, raw, wrapped)


def shifted(tiles, t, by):
    count = len(tiles)
    if by > 0:
        joined = jnp.where(lane_index() < by, tiles[(t + 1) % count], tiles[t])
    else:
        joined = jnp.where(lane_index() >= LANES + by, tiles[(t - 1) % count], tiles[t])
    return pltpu.roll(joined, (-by) % LANES, 1)


def mirrored(tiles, rem):
    lane = lane_index()
    index = (rem - 1 - lane) % LANES
    turned = [jnp.take_along_axis(tile, index, axis=1, mode="promise_in_bounds") for tile in tiles]
    last = len(tiles) - 1
    out = [jnp.where(lane < rem, turned[last - t], turned[last - 1 - t]) for t in range(last)]
    return [*out, turned[0]]


def natural_tile(ref, where, t, lon):
    full, rem = divmod(lon, LANES)
    if t < full:
        return ref[(*where, slice(None), pl.ds(t * LANES, LANES))]
    tail = ref[(*where, slice(None), pl.ds(full * LANES, rem))]
    head = ref[(*where, slice(None), pl.ds(0, LANES))][:, : LANES - 2 * rem]
    return jnp.concatenate([tail, head, tail], axis=1)


def stage_currents(currents, levels, held, lon):
    tiles = lon // LANES + 1
    for t in range(tiles):
        for c in range(2):
            for half in range(2):
                pair = [natural_tile(currents, (c, 2 * half + k), t, lon) for k in range(2)]
                held[pl.ds((t * 5 + 2 * c + half) * 8, 8), :] = jnp.concatenate(pair, axis=0)
        column = natural_tile(levels, (), t, lon).astype(jnp.float32)
        held[pl.ds((t * 5 + 4) * 8, 8), :] = jnp.concatenate([column, column], axis=0)


def own_row(held, t, c, row):
    return held[pl.ds((t * 5 + 2 * c) * 8 + row, 4, stride=4), :]


def edge_rows(held, out, base, north, lon):
    u0, v0 = jnp.where(north, 2, 0), jnp.where(north, 1, 0)
    for t in range(lon // LANES + 1):
        u = [own_row(held, t, 0, u0 + k) for k in range(2)]
        v = [own_row(held, t, 1, v0 + k) for k in range(3)]
        column = held[pl.ds((t * 5 + 4) * 8, 4), :]
        start = base + t * SMALL
        out[pl.ds(start, 8), :] = jnp.concatenate(u, axis=0)
        out[pl.ds(start + 8, 8), :] = jnp.concatenate(v[:2], axis=0)
        out[pl.ds(start + 16, 8), :] = jnp.concatenate([v[2], column], axis=0)


def folded_edge_rows(held, out, base, lon):
    tiles, rem = lon // LANES + 1, lon % LANES

    def write(row, pieces):
        folded = mirrored([jnp.concatenate([p(t) for p in pieces], axis=0) for t in range(tiles)], rem)
        folded[-1] = wrap_tile(folded[-1], folded[0], rem)
        for t in range(tiles):
            out[pl.ds(base + t * SMALL + row, 8), :] = folded[t]

    def current(c, row):
        return lambda t: -own_row(held, t, c, row)

    def column(row):
        return lambda t: held[pl.ds((t * 5 + 4) * 8 + row, 1), :]

    write(0, [current(0, 3), current(0, 2)])
    write(8, [current(1, 3), current(1, 2)])
    write(16, [current(1, 1)] + [column(3 - k) for k in range(4)])


def pack_kernel(offset, n, lon, small, *refs):
    if small:
        x_hbm, c_hbm, l_hbm, to_far, to_near, near_small, x, tail, sem, currents, levels, held, sems = refs
    else:
        x_hbm, to_far, to_near, x, tail, sem = refs
    full, rem = divmod(lon, LANES)
    size = (16 * full + 4) * n
    place = lax.axis_index("lat")
    top = place == lax.axis_size("lat") - 1
    copy = pltpu.make_async_copy(x_hbm.at[pl.ds(offset, n)], x, sem)
    if small:
        copies = [pltpu.make_async_copy(c_hbm, currents, sems.at[0]), pltpu.make_async_copy(l_hbm, levels, sems.at[1])]
        for c in copies:
            c.start()
        copy.start()
        odd = place % 2 == 1
        for c in copies:
            c.wait()
        stage_currents(currents, levels, held, lon)
        edge_rows(held, near_small, 0, jnp.logical_not(odd), lon)

        @pl.when(jnp.logical_not(top))
        def _():
            edge_rows(held, to_far, size, odd, lon)

        @pl.when(top)
        def _():
            folded_edge_rows(held, to_far, size, lon)
    else:
        copy.start()
    copy.wait()
    lane = lane_index()

    def joined(rests):
        out = rests[3]
        for r in range(3):
            out = jnp.where((lane >= r * rem) & (lane < (r + 1) * rem), rests[r], out)
        return out

    def pair(g, carry):
        first = pl.multiple_of(g * (32 * full), 8)
        for k in range(2):
            for level in range(4):
                for t in range(full):
                    tile = x[2 * g + k, level, :, pl.ds(t * LANES, LANES)]
                    to_near[pl.ds(first + t * 8 + 4 * k + level, 4, stride=full * 8), :] = tile
                rest = x[2 * g + k, level, :, pl.ds(full * LANES, rem)]
                tail[pl.ds(4 * k + level, 4, stride=8), :] = jnp.concatenate([rest] * (LANES // rem), axis=1)
        end = pl.multiple_of(16 * full * n + 8 * g, 8)
        to_near[pl.ds(end, 8), :] = joined([tail[pl.ds(8 * r, 8), :] for r in range(4)])

        @pl.when(jnp.logical_not(top))
        def _():
            for j in range(4 * full):
                to_far[pl.ds(first + j * 8, 8), :] = to_near[pl.ds(first + j * 8, 8), :]
            to_far[pl.ds(end, 8), :] = to_near[pl.ds(end, 8), :]

        @pl.when(top)
        def _():
            rests = []
            for r in range(4):
                source = 3 - r
                row = [to_near[pl.ds(first + (source * full + t) * 8, 8), :] for t in range(full)]
                row.append(tail[pl.ds(8 * source, 8), :])
                folded = mirrored(row, rem)
                for t in range(full):
                    to_far[pl.ds(first + (r * full + t) * 8, 8), :] = folded[t]
                rests.append(pltpu.roll(folded[full], r * rem, 1) if r else folded[full])
            to_far[pl.ds(end, 8), :] = joined(rests)

        return carry

    lax.fori_loop(0, n // 2, pair, 0)


def coefficient_kernel(n, lon, currents, levels, near, far, k1, k2, held, u, v, w):
    full, _ = divmod(lon, LANES)
    tiles = full + 1
    far_base = (16 * full + 4) * n
    place = lax.axis_index("lat")
    odd = place % 2 == 1
    level = (lax.broadcasted_iota(jnp.int32, (8, LANES), 0) % 4).astype(jnp.float32)
    stage_currents(currents, levels, held, lon)

    def put(dst, row, t, value):
        dst[pl.ds((row * tiles + t) * 8, 8), :] = value

    def get(src, row):
        return [src[pl.ds((row * tiles + t) * 8, 8), :] for t in range(tiles)]

    def twice(value):
        return jnp.concatenate([value, value], axis=0)

    for t in range(tiles):
        for row in range(4):
            put(u, 2 + row, t, twice(own_row(held, t, 0, row)))
            put(v, 3 + row, t, twice(own_row(held, t, 1, row)))
            column = spread(held, (t * 5 + 4) * 8 + row)
            put(w, 4 + row, t, (level < column).astype(jnp.float32))
        sides = ((0, 0, 0, True), (6, 7, 8, False))
        for u_row, v_row, w_row, is_low in sides:
            take_near = odd if is_low else jnp.logical_not(odd)

            def pick(start, size):
                a = near[pl.ds(t * SMALL + start, size), :]
                b = far[pl.ds(far_base + t * SMALL + start, size), :]
                return jnp.where(take_near, a, b)

            for k in range(2):
                put(u, u_row + k, t, twice(pick(4 * k, 4)))
            for k in range(3):
                put(v, v_row + k, t, twice(pick(8 + 4 * k, 4)))
            for k in range(4):
                put(w, w_row + k, t, (level < jnp.broadcast_to(pick(20 + k, 1), level.shape)).astype(jnp.float32))

    def parts(face):
        return jnp.maximum(face, 0.0) * (1.0 / 6.0), jnp.minimum(face, 0.0) * (1.0 / 6.0)

    def north_faces(row):
        wa, wb, va, vb = get(w, row + 4), get(w, row + 5), get(v, row + 3), get(v, row + 4)
        return [parts(wa[t] * wb[t] * (0.5 * (va[t] + vb[t]))) for t in range(tiles)]

    south = north_faces(-3)
    for row in range(-2, 6):
        north = north_faces(row)
        ur = get(u, row + 2)
        wr = {d: get(w, row + 4 + d) for d in (-2, -1, 0, 1, 2)}
        we = {d: [shifted(wr[0], t, d) for t in range(tiles)] for d in (-2, -1, 1, 2)}
        east = [parts(wr[0][t] * we[1][t] * (0.5 * (ur[t] + shifted(ur, t, 1)))) for t in range(tiles)]
        west_p = [shifted([e[0] for e in east], t, -1) for t in range(tiles)]
        west_m = [shifted([e[1] for e in east], t, -1) for t in range(tiles)]
        for t in range(tiles):
            (p, m), (q, s), (qs, ss) = east[t], north[t], south[t]
            pw, mw = west_p[t], west_m[t]
            plain = [
                -pw,
                p + 5.0 * pw + 2.0 * mw,
                -(2.0 * p + 5.0 * m + mw),
                m,
                1.0 - (5.0 * p + 2.0 * m) + (2.0 * pw + 5.0 * mw) - (5.0 * q + 2.0 * s) + (2.0 * qs + 5.0 * ss),
                -qs,
                q + 5.0 * qs + 2.0 * ss,
                -(2.0 * q + 5.0 * s + ss),
                s,
            ]
            source = [we[-2][t], we[-1][t], we[1][t], we[2][t], wr[0][t], wr[-2][t], wr[-1][t], wr[1][t], wr[2][t]]
            here = wr[0][t]
            half = 0.5 * here
            at1 = jnp.where(odd, row + 2, 5 - row) * (tiles * 9 * 8)
            at2 = jnp.where(odd, row, 3 - row) * (tiles * 10 * 8)
            for k in range(9):
                turn = k if k < 5 else jnp.where(odd, k, 13 - k)
                start = pl.multiple_of(at1 + (t * 9 + turn) * 8, 8)
                k1[pl.ds(start, 8), :] = plain[k] * source[k] * here
                if 0 <= row < 4:
                    start = pl.multiple_of(at2 + (t * 10 + turn) * 8, 8)
                    k2[pl.ds(start, 8), :] = plain[k] * half
            if 0 <= row < 4:
                start = pl.multiple_of(at2 + (t * 10 + 9) * 8, 8)
                k2[pl.ds(start, 8), :] = half * here
        south = north


def stencil(coefficients, here, before, after, rows):
    tiles = [here, after, before]
    values = [shifted(tiles, 0, d) for d in (-2, -1, 1, 2)] + [here] + rows
    total = coefficients[0] * values[0]
    for k in range(1, 9):
        total = total + coefficients[k] * values[k]
    return total


def advect_kernel(n, lon, groups, own, near, far, k1, k2, *refs):
    out, last, first, turned = refs[-4:]
    full, rem = divmod(lon, LANES)
    tiles = full + 1
    odd = lax.axis_index("lat") % 2 == 1
    group0 = pl.program_id(0) * groups
    physical = [jnp.where(odd, j, 3 - j) for j in range(4)]

    starts = [[pl.multiple_of((4 * (group0 + i) + physical[j]) * (full * 8), 8) for j in range(4)] for i in range(groups)]
    for i in range(groups):
        for side, source in enumerate((near, own, far)):
            rest = source[pl.ds(pl.multiple_of(16 * full * n + 8 * (group0 + i), 8), 8), :]
            for j in range(4):
                raw = pltpu.roll(rest, jnp.where(odd, (-j * rem) % LANES, ((j - 3) * rem) % LANES), 1)
                begin = source[pl.ds(starts[i][j], 8), :]
                last[pl.ds((i * 12 + side * 4 + j) * 8, 8), :] = wrap_tile(raw, begin, rem)

    def f(i, row, t):
        t = t % tiles
        side, j = divmod(row + 4, 4)
        if t == full:
            return last[pl.ds((i * 12 + side * 4 + j) * 8, 8), :]
        return (near, own, far)[side][pl.ds(starts[i][j] + t * 8, 8), :]

    def once(i, row, t):
        return ((i * 8 + row + 2) * tiles + t % tiles) * 8

    for t in range(tiles):
        column = [[f(i, row, t) for row in range(-4, 8)] for i in range(groups)]
        for row in range(-2, 6):
            base = ((row + 2) * tiles + t) * 9
            coefficients = [k1[pl.ds((base + k) * 8, 8), :] for k in range(9)]
            for i in range(groups):
                c = column[i]
                rows = [c[row + 4 + d] for d in (-2, -1, 1, 2)]
                value = stencil(coefficients, c[row + 4], f(i, row, t - 1), f(i, row, t + 1), rows)
                first[pl.ds(once(i, row, t), 8), :] = value

    for t in range(tiles):
        column = [[first[pl.ds(once(i, row, t), 8), :] for row in range(-2, 6)] for i in range(groups)]
        for row in range(4):
            base = (row * tiles + t) * 10
            coefficients = [k2[pl.ds((base + k) * 8, 8), :] for k in range(10)]
            for i in range(groups):
                c = column[i]
                rows = [c[row + 2 + d] for d in (-2, -1, 1, 2)]
                before, after = (first[pl.ds(once(i, row, t + d), 8), :] for d in (-1, 1))
                value = stencil(coefficients, c[row + 2], before, after, rows) + coefficients[9] * f(i, row, t)
                turned[pl.ds((i * tiles + t) * 32 + physical[row], 8, stride=4), :] = value
        for i in range(groups):
            for k in range(2):
                for level in range(4):
                    value = turned[pl.ds((i * tiles + t) * 32 + (4 * k + level) * 4, 4), :]
                    if t < full:
                        out[2 * i + k, level, :, pl.ds(t * LANES, LANES)] = value
                    else:
                        out[2 * i + k, level, :, pl.ds(full * LANES, rem)] = value[:, :rem]


def vmem():
    return pl.BlockSpec(memory_space=pltpu.VMEM)


def shards(tracers, currents, column_levels):
    count = lax.axis_size("lat")
    total, levels, rows, lon = tracers.shape
    full, rem = divmod(lon, LANES)
    tiles = full + 1
    assert levels == 4 and rows == 4 and 4 * rem == LANES and count % 2 == 0 and sum(CHUNKS) == total
    near_pairs = [(i, i ^ 1) for i in range(count)]
    far_pairs = [pair for i in range(1, count - 1, 2) for pair in ((i, i + 1), (i + 1, i))]
    far_pairs.append((count - 1, count - 1))
    f32 = jnp.float32

    packed, kept, near_small = [], [], None
    for i, (offset, n) in enumerate(zip(OFFSETS, CHUNKS)):
        small = i == 0
        size = (16 * full + 4) * n
        shape = [
            jax.ShapeDtypeStruct((size + (SMALL * tiles if small else 0), LANES), f32),
            jax.ShapeDtypeStruct((size, LANES), f32),
        ]
        scratch = [pltpu.VMEM((n, levels, rows, lon), f32), pltpu.VMEM((32, LANES), f32), pltpu.SemaphoreType.DMA]
        if small:
            shape.append(jax.ShapeDtypeStruct((SMALL * tiles, LANES), f32))
            scratch += [
                pltpu.VMEM(currents.shape, f32),
                pltpu.VMEM(column_levels.shape, jnp.int32),
                pltpu.VMEM((tiles * 40, LANES), f32),
                pltpu.SemaphoreType.DMA((2,)),
            ]
        result = pl.pallas_call(
            functools.partial(pack_kernel, offset, n, lon, small),
            out_shape=shape,
            in_specs=[pl.BlockSpec(memory_space=pltpu.HBM)] * (3 if small else 1),
            out_specs=[vmem() for _ in shape],
            scratch_shapes=scratch,
            cost_estimate=pl.CostEstimate(flops=1000000 * n, bytes_accessed=n * 184320, transcendentals=0),
            compiler_params=pltpu.CompilerParams(vmem_limit_bytes=16 * 2**20),
        )(tracers, *((currents, column_levels) if small else ()))
        packed.append(result[0])
        kept.append(result[1])
        if small:
            near_small = result[2]
    far = []
    for i in range(len(CHUNKS)):
        far.append(lax.ppermute(packed[i], "lat", far_pairs))
    small_received = lax.ppermute(near_small, "lat", near_pairs)
    near = []
    for i in range(len(CHUNKS)):
        near.append(lax.ppermute(kept[i], "lat", near_pairs))
    k1, k2 = pl.pallas_call(
        functools.partial(coefficient_kernel, CHUNKS[0], lon),
        out_shape=[
            jax.ShapeDtypeStruct((8 * tiles * 9 * 8, LANES), f32),
            jax.ShapeDtypeStruct((4 * tiles * 10 * 8, LANES), f32),
        ],
        in_specs=[vmem()] * 4,
        out_specs=[vmem()] * 2,
        scratch_shapes=[
            pltpu.VMEM((tiles * 40, LANES), f32),
            pltpu.VMEM((8 * tiles * 8, LANES), f32),
            pltpu.VMEM((10 * tiles * 8, LANES), f32),
            pltpu.VMEM((12 * tiles * 8, LANES), f32),
        ],
        cost_estimate=pl.CostEstimate(flops=8000000, bytes_accessed=6000000, transcendentals=0),
        compiler_params=pltpu.CompilerParams(vmem_limit_bytes=20 * 2**20),
        name="coefficients",
    )(currents, column_levels, small_received, far[0])
    out = None
    for i, (offset, n, groups) in enumerate(zip(OFFSETS, CHUNKS, GROUPS)):
        operands = [kept[i], near[i], far[i], k1, k2]
        specs = [vmem()] * 5
        aliases = {}
        if out is not None:
            aliases = {len(operands): 0}
            operands.append(out)
            specs.append(pl.BlockSpec(memory_space=pl.ANY))
        out = pl.pallas_call(
            functools.partial(advect_kernel, n, lon, groups),
            out_shape=jax.ShapeDtypeStruct(tracers.shape, f32),
            grid=(n // (2 * groups),),
            in_specs=specs,
            out_specs=pl.BlockSpec(
                (2 * groups, levels, rows, lon), lambda g, o=offset // (2 * groups): (o + g, 0, 0, 0)
            ),
            scratch_shapes=[
                pltpu.VMEM((groups * 12 * 8, LANES), f32),
                pltpu.VMEM((groups * 8 * tiles * 8, LANES), f32),
                pltpu.VMEM((groups * 32 * tiles, LANES), f32),
            ],
            input_output_aliases=aliases,
            cost_estimate=pl.CostEstimate(flops=3000000 * n, bytes_accessed=n * 500000, transcendentals=0),
            compiler_params=pltpu.CompilerParams(vmem_limit_bytes=24 * 2**20),
        )(*operands)
    return out


def solution(mesh):
    in_specs = (
        P("member", None, "lat", None),
        P("member", None, "lat", None),
        P(("member", "lat"), None),
    )
    out_specs = P("member", None, "lat", None)
    return jax.shard_map(shards, mesh=mesh, in_specs=in_specs, out_specs=out_specs, check_vma=False)
```

time: 75 us -> 57.8 us (0.77)
  waiting for transfers between devices: 22.9 us -> 0.85 us
  Pallas kernels: 21.1 us -> 23 us
  local copies, waits for them, and re-layouts: 1.84 us -> 3.51 us
  starting transfers between devices: 28.8 us -> 29.9 us
    ppermute x3 -> x4, waiting for transfers between devices: 21.2 us -> 0.01 us  [shards(): far.append(lax.ppermute(packed[i], 'lat', far_pairs))]
    ppermute x3 -> x4, starting transfers between devices: 7.55 us -> 12.7 us  [shards(): far.append(lax.ppermute(packed[i], 'lat', far_pairs))]
    ppermute x3 -> x4, starting transfers between devices: 20.8 us -> 17.1 us  [shards(): near.append(lax.ppermute(kept[i], 'lat', near_pairs))]
    unnamed x6 -> x10, local copies, waits for them, and re-layouts: 1.84 us -> 3.51 us
    pallas_call x3 -> x4, Pallas kernels: 1.53 us -> 2.89 us  [shards(): pl.pallas_call(functools.partial(pack_kernel, offset, n, lon, small), out...]
    ppermute x1, waiting for transfers between devices: 1.77 us -> 0.83 us  [shards(): small_received = lax.ppermute(near_small, 'lat', near_pairs)]
    pallas_call x3 -> x4, Pallas kernels: 17.9 us -> 18.7 us  [shards(): pl.pallas_call(functools.partial(advect_kernel, n, lon, groups), out_shap...]
  transfers between devices with their start and end apart: 7 -> 9, of which waited for: 2 -> 1; matrix products, arithmetic and copies ran while one was open for 0% -> 0% of each run, Pallas kernels for 22% -> 33%
where the time goes in v2:
time: 57.8 us; the launch traced here: 57.5 us
  starting transfers between devices  29.9 us (52%)
  Pallas kernels  23 us (40%)
  local copies, waits for them, and re-layouts  3.51 us (6%)
  waiting for transfers between devices  0.85 us (1%)
    pallas_call x4, Pallas kernels, shards(): pl.pallas_call(functools.partial(advect_kernel, n, lon, groups), out_shap...  18.7 us
    ppermute x4, starting transfers between devices, shards(): near.append(lax.ppermute(kept[i], 'lat', near_pairs))  17.1 us
    ppermute x4, starting transfers between devices, shards(): far.append(lax.ppermute(packed[i], 'lat', far_pairs))  12.7 us
    unnamed x10, local copies, waits for them, and re-layouts  3.51 us
    pallas_call x4, Pallas kernels, shards(): pl.pallas_call(functools.partial(pack_kernel, offset, n, lon, small), out...  2.89 us
    pallas_call x1, Pallas kernels, shards(): pl.pallas_call(functools.partial(coefficient_kernel, CHUNKS[0], lon), out...  1.46 us
  transfers between devices with their start and end apart: 9, of which 1 were waited for; matrix products, arithmetic and copies ran while one was open for 0% of the time, Pallas kernels for 33%

profile of v2, /device:TPU:33, one launch (start us, length us, event | category | flops | bytes accessed | tf_op | source)
XLA Modules:
  0.0 57.5 jit_solution(7571350251858231027)
XLA Ops:
  0.0 0.0 copy-start
  0.0 1.8 %copy-done = f32[30,4,4,1440]{3,2,1,0:T(4,128)S(1)} copy-done((f32[30,4,4,1440]{3,2,1,0:T(4,128)S(1)}, f32[30,4,4,1440]{3,2,1,0:T(4,128)}, u32[]{:S(2)}) %copy-start) | copy-done | bytes 2764824
  1.8 0.0 copy-start.1
  1.8 0.9 %copy-done.1 = f32[2,4,4,1440]{3,2,1,0:T(4,128)S(1)} copy-done((f32[2,4,4,1440]{3,2,1,0:T(4,128)S(1)}, f32[2,4,4,1440]{3,2,1,0:T(4,128)}, u32[]{:S(2)}) %copy-start.1) | copy-done | bytes 184344
  2.8 0.0 copy-start.3
  2.8 0.7 %copy-done.3 = s32[4,1440]{1,0:T(4,128)S(1)} copy-done((s32[4,1440]{1,0:T(4,128)S(1)}, s32[4,1440]{1,0:T(4,128)}, u32[]{:S(2)}) %copy-start.3) | copy-done | bytes 23064
  3.5 1.4 %shard_map.38 = (f32[2448,128]{1,0:T(8,128)S(1)}, f32[2160,128]{1,0:T(8,128)S(1)}, f32[288,128]{1,0:T(8,128)S(1)}) custom-call(f32[30,4,4,1440]{3,2,1,0:T(4,128)S(1)} %copy-done, f32[2,4,4,1440]{3,2,1,0:T(4,128)S(1)} %copy-done.1, s32[4,1440]{1,0:T(4,128)S(1)} %copy-done.3), custom_call_target="tpu_custom_call" | custom-call | flops 12000000 | bytes 2211840 | tf_op jit(solution)/shard_map/pallas_call | solution.py:371
  4.9 4.6 %collective-permute-start.3 = (f32[2448,128]{1,0:T(8,128)S(1)}, f32[2448,128]{1,0:T(8,128)S(1)}, u32[]{:S(2)}, u32[]{:S(2)}) collective-permute-start(f32[2448,128]{1,0:T(8,128)S(1)} %get-tuple-element.19), channel_id=1, source_target_pairs={{1,2},{2,1},{3,4},{4,3},{5,6},{6,5},{7,8},{8,7},{9,10},{10,9},{11,... | collective-permute-start | bytes 3760136 | tf_op jit(solution)/shard_map/ppermute | solution.py:386
  9.5 16.7 %collective-permute-start.8 = (f32[2160,128]{1,0:T(8,128)S(1)}, f32[2160,128]{1,0:T(8,128)S(1)}, u32[]{:S(2)}, u32[]{:S(2)}) collective-permute-start(f32[2160,128]{1,0:T(8,128)S(1)} %get-tuple-element.26.own), channel_id=1, source_target_pairs={{0,1},{1,0},{2,3},{3,2},{4,5},{5,4},{6,7},{7,6},{8,9},{9,8},{10,11... | collective-permute-start | bytes 3317768 | tf_op jit(solution)/shard_map/ppermute | solution.py:390
  26.2 0.6 shard_map.40
  26.7 0.2 collective-permute-start.6
  26.9 1.9 %collective-permute-start.7 = (f32[1440,128]{1,0:T(8,128)S(1)}, f32[1440,128]{1,0:T(8,128)S(1)}, u32[]{:S(2)}, u32[]{:S(2)}) collective-permute-start(f32[1440,128]{1,0:T(8,128)S(1)} %get-tuple-element.25), channel_id=1, source_target_pairs={{1,2},{2,1},{3,4},{4,3},{5,6},{6,5},{7,8},{8,7},{9,10},{10,9},{11,... | collective-permute-start | bytes 2211848 | tf_op jit(solution)/shard_map/ppermute | solution.py:386
  28.8 0.0 copy-start.2
  28.9 0.0 copy-start.4
  28.9 0.1 collective-permute-start.2
  29.0 0.5 shard_map.39
  29.5 0.8 %collective-permute-done.2.near = f32[288,128]{1,0:T(8,128)S(1)} collective-permute-done((f32[288,128]{1,0:T(8,128)S(1)}, f32[288,128]{1,0:T(8,128)S(1)}, u32[]{:S(2)}, u32[]{:S(2)}) %collective-permute-start.2) | collective-permute-done | bytes 147488 | tf_op jit(solution)/shard_map/ppermute | solution.py:387
  30.4 0.1 collective-permute-start.4
  30.5 0.0 collective-permute-done.6.near
  30.5 3.7 %collective-permute-start.5 = (f32[1080,128]{1,0:T(8,128)S(1)}, f32[1080,128]{1,0:T(8,128)S(1)}, u32[]{:S(2)}, u32[]{:S(2)}) collective-permute-start(f32[1080,128]{1,0:T(8,128)S(1)} %get-tuple-element.23), channel_id=1, source_target_pairs={{1,2},{2,1},{3,4},{4,3},{5,6},{6,5},{7,8},{8,7},{9,10},{10,9},{11,... | collective-permute-start | bytes 1658888 | tf_op jit(solution)/shard_map/ppermute | solution.py:386
  34.2 0.5 shard_map.37
  34.6 0.0 collective-permute-done.8.near
  34.7 0.1 collective-permute-start
  34.8 0.0 collective-permute-done.3.far
  34.8 2.5 %collective-permute-start.1 = (f32[720,128]{1,0:T(8,128)S(1)}, f32[720,128]{1,0:T(8,128)S(1)}, u32[]{:S(2)}, u32[]{:S(2)}) collective-permute-start(f32[720,128]{1,0:T(8,128)S(1)} %get-tuple-element.17), channel_id=1, source_target_pairs={{1,2},{2,1},{3,4},{4,3},{5,6},{6,5},{7,8},{8,7},{9,10},{10,9},{11,... | collective-permute-start | bytes 1105928 | tf_op jit(solution)/shard_map/ppermute | solution.py:386
  37.3 0.0 copy-done.2
  37.3 0.0 copy-done.4
  37.3 1.5 %coefficients.1 = (f32[6912,128]{1,0:T(8,128)S(1)}, f32[3840,128]{1,0:T(8,128)S(1)}) custom-call(f32[2,4,4,1440]{3,2,1,0:T(4,128)S(1)} %copy-done.2, s32[4,1440]{1,0:T(4,128)S(1)} %copy-done.4, f32[288,128]{1,0:T(8,128)S(1)} %collective-permute-done.2.near, f32[2448,128]{1,0:T(8,128)S(1)} %collective-permute-done.3.far), custom_call_target="tpu_custom_call" | custom-call | flops 8000000 | bytes 6000000 | tf_op jit(solution)/shard_map/coefficients/pallas_call | solution.py:391
  38.8 7.3 %shard_map.41.refs_0_ = f32[30,4,4,1440]{3,2,1,0:T(4,128)} custom-call(f32[2160,128]{1,0:T(8,128)S(1)} %get-tuple-element.26.own, f32[2160,128]{1,0:T(8,128)S(1)} %collective-permute-done.8.near, f32[2448,128]{1,0:T(8,128)S(1)} %collective-permute-done.3.far, f32[6912,128]{1,0:T(8,128)S(1)} %get-tuple-element.20.k1, f32[3840,128]{1,0:T(8,128)S(1)} %get-tuple-element.21.k2), custom_call_target="tpu_custom_call" | custom-call | flops 36000000 | bytes 6000000 | tf_op jit(solution)/shard_map/pallas_call | solution.py:418
  46.1 0.0 collective-permute-done.7.far
  46.1 4.7 %shard_map.42.refs_0_ = f32[30,4,4,1440]{3,2,1,0:T(4,128)} custom-call(f32[1440,128]{1,0:T(8,128)S(1)} %get-tuple-element.24.own, f32[1440,128]{1,0:T(8,128)S(1)} %collective-permute-done.6.near, f32[1440,128]{1,0:T(8,128)S(1)} %collective-permute-done.7.far, f32[6912,128]{1,0:T(8,128)S(1)} %get-tuple-element.20.k1, ...), custom_call_target="tpu_custom_call", output_to_operand_aliasing={{}: (5, {})} | custom-call | flops 24000000 | bytes 4000000 | tf_op jit(solution)/shard_map/pallas_call | solution.py:418
  50.8 0.0 collective-permute-done.4.near
  50.8 0.0 collective-permute-done.5.far
  50.8 4.0 %shard_map.43.refs_0_ = f32[30,4,4,1440]{3,2,1,0:T(4,128)} custom-call(f32[1080,128]{1,0:T(8,128)S(1)} %get-tuple-element.22.own, f32[1080,128]{1,0:T(8,128)S(1)} %collective-permute-done.4.near, f32[1080,128]{1,0:T(8,128)S(1)} %collective-permute-done.5.far, f32[6912,128]{1,0:T(8,128)S(1)} %get-tuple-element.20.k1, ...), custom_call_target="tpu_custom_call", output_to_operand_aliasing={{}: (5, {})} | custom-call | flops 18000000 | bytes 3000000 | tf_op jit(solution)/shard_map/pallas_call | solution.py:418
  54.8 0.0 collective-permute-done.near
  54.8 0.0 collective-permute-done.1.far
  54.8 2.7 %shard_map.44 = f32[30,4,4,1440]{3,2,1,0:T(4,128)} custom-call(f32[720,128]{1,0:T(8,128)S(1)} %get-tuple-element.16.own, f32[720,128]{1,0:T(8,128)S(1)} %collective-permute-done.near, f32[720,128]{1,0:T(8,128)S(1)} %collective-permute-done.1.far, f32[6912,128]{1,0:T(8,128)S(1)} %get-tuple-element.20.k1, ...), custom_call_target="tpu_custom_call", output_to_operand_aliasing={{}: (5, {})} | custom-call | flops 12000000 | bytes 2000000 | tf_op jit(solution)/shard_map/pallas_call | solution.py:418
Async XLA Ops:
  0.0 1.8 %copy-start = (f32[30,4,4,1440]{3,2,1,0:T(4,128)S(1)}, f32[30,4,4,1440]{3,2,1,0:T(4,128)}, u32[]{:S(2)}) copy-start(f32[30,4,4,1440]{3,2,1,0:T(4,128)} %refs_0_.7) | copy-start | bytes 8294404
  1.8 0.9 %copy-start.1 = (f32[2,4,4,1440]{3,2,1,0:T(4,128)S(1)}, f32[2,4,4,1440]{3,2,1,0:T(4,128)}, u32[]{:S(2)}) copy-start(f32[2,4,4,1440]{3,2,1,0:T(4,128)} %currents.1) | copy-start | bytes 552964
  2.8 0.7 %copy-start.3 = (s32[4,1440]{1,0:T(4,128)S(1)}, s32[4,1440]{1,0:T(4,128)}, u32[]{:S(2)}) copy-start(s32[4,1440]{1,0:T(4,128)} %levels.1) | copy-start | bytes 69124
  4.9 29.9 %collective-permute-start.3 = (f32[2448,128]{1,0:T(8,128)S(1)}, f32[2448,128]{1,0:T(8,128)S(1)}, u32[]{:S(2)}, u32[]{:S(2)}) collective-permute-start(f32[2448,128]{1,0:T(8,128)S(1)} %get-tuple-element.19), channel_id=1, source_target_pairs={{1,2},{2,1},{3,4},{4,3},{5,6},{6,5},{7,8},{8,7},{9,10},{10,9},{11,... | collective-permute-start | bytes 3760136 | tf_op jit(solution)/shard_map/ppermute | solution.py:386
  9.5 25.2 %collective-permute-start.8 = (f32[2160,128]{1,0:T(8,128)S(1)}, f32[2160,128]{1,0:T(8,128)S(1)}, u32[]{:S(2)}, u32[]{:S(2)}) collective-permute-start(f32[2160,128]{1,0:T(8,128)S(1)} %get-tuple-element.26.own), channel_id=1, source_target_pairs={{0,1},{1,0},{2,3},{3,2},{4,5},{5,4},{6,7},{7,6},{8,9},{9,8},{10,11... | collective-permute-start | bytes 3317768 | tf_op jit(solution)/shard_map/ppermute | solution.py:390
  26.7 3.8 %collective-permute-start.6 = (f32[1440,128]{1,0:T(8,128)S(1)}, f32[1440,128]{1,0:T(8,128)S(1)}, u32[]{:S(2)}, u32[]{:S(2)}) collective-permute-start(f32[1440,128]{1,0:T(8,128)S(1)} %get-tuple-element.24.own), channel_id=1, source_target_pairs={{0,1},{1,0},{2,3},{3,2},{4,5},{5,4},{6,7},{7,6},{8,9},{9,8},{10,11... | collective-permute-start | bytes 2211848 | tf_op jit(solution)/shard_map/ppermute | solution.py:390
  26.9 19.2 %collective-permute-start.7 = (f32[1440,128]{1,0:T(8,128)S(1)}, f32[1440,128]{1,0:T(8,128)S(1)}, u32[]{:S(2)}, u32[]{:S(2)}) collective-permute-start(f32[1440,128]{1,0:T(8,128)S(1)} %get-tuple-element.25), channel_id=1, source_target_pairs={{1,2},{2,1},{3,4},{4,3},{5,6},{6,5},{7,8},{8,7},{9,10},{10,9},{11,... | collective-permute-start | bytes 2211848 | tf_op jit(solution)/shard_map/ppermute | solution.py:386
  28.8 8.4 %copy-start.2 = (f32[2,4,4,1440]{3,2,1,0:T(4,128)S(1)}, f32[2,4,4,1440]{3,2,1,0:T(4,128)}, u32[]{:S(2)}) copy-start(f32[2,4,4,1440]{3,2,1,0:T(4,128)} %currents.1) | copy-start | bytes 552964
  28.9 8.4 %copy-start.4 = (s32[4,1440]{1,0:T(4,128)S(1)}, s32[4,1440]{1,0:T(4,128)}, u32[]{:S(2)}) copy-start(s32[4,1440]{1,0:T(4,128)} %levels.1) | copy-start | bytes 69124
  28.9 1.5 %collective-permute-start.2 = (f32[288,128]{1,0:T(8,128)S(1)}, f32[288,128]{1,0:T(8,128)S(1)}, u32[]{:S(2)}, u32[]{:S(2)}) collective-permute-start(f32[288,128]{1,0:T(8,128)S(1)} %get-tuple-element.18), channel_id=1, source_target_pairs={{0,1},{1,0},{2,3},{3,2},{4,5},{5,4},{6,7},{7,6},{8,9},{9,8},{10,11... | collective-permute-start | bytes 442376 | tf_op jit(solution)/shard_map/ppermute | solution.py:387
  30.4 20.4 %collective-permute-start.4 = (f32[1080,128]{1,0:T(8,128)S(1)}, f32[1080,128]{1,0:T(8,128)S(1)}, u32[]{:S(2)}, u32[]{:S(2)}) collective-permute-start(f32[1080,128]{1,0:T(8,128)S(1)} %get-tuple-element.22.own), channel_id=1, source_target_pairs={{0,1},{1,0},{2,3},{3,2},{4,5},{5,4},{6,7},{7,6},{8,9},{9,8},{10,11... | collective-permute-start | bytes 1658888 | tf_op jit(solution)/shard_map/ppermute | solution.py:390
  30.5 20.2 %collective-permute-start.5 = (f32[1080,128]{1,0:T(8,128)S(1)}, f32[1080,128]{1,0:T(8,128)S(1)}, u32[]{:S(2)}, u32[]{:S(2)}) collective-permute-start(f32[1080,128]{1,0:T(8,128)S(1)} %get-tuple-element.23), channel_id=1, source_target_pairs={{1,2},{2,1},{3,4},{4,3},{5,6},{6,5},{7,8},{8,7},{9,10},{10,9},{11,... | collective-permute-start | bytes 1658888 | tf_op jit(solution)/shard_map/ppermute | solution.py:386
  34.7 20.1 %collective-permute-start = (f32[720,128]{1,0:T(8,128)S(1)}, f32[720,128]{1,0:T(8,128)S(1)}, u32[]{:S(2)}, u32[]{:S(2)}) collective-permute-start(f32[720,128]{1,0:T(8,128)S(1)} %get-tuple-element.16.own), channel_id=1, source_target_pairs={{0,1},{1,0},{2,3},{3,2},{4,5},{5,4},{6,7},{7,6},{8,9},{9,8},{10,11... | collective-permute-start | bytes 1105928 | tf_op jit(solution)/shard_map/ppermute | solution.py:390
  34.8 20.0 %collective-permute-start.1 = (f32[720,128]{1,0:T(8,128)S(1)}, f32[720,128]{1,0:T(8,128)S(1)}, u32[]{:S(2)}, u32[]{:S(2)}) collective-permute-start(f32[720,128]{1,0:T(8,128)S(1)} %get-tuple-element.17), channel_id=1, source_target_pairs={{1,2},{2,1},{3,4},{4,3},{5,6},{6,5},{7,8},{8,7},{9,10},{10,9},{11,... | collective-permute-start | bytes 1105928 | tf_op jit(solution)/shard_map/ppermute | solution.py:386

commit v3 on v2

--- a/solution.py
+++ b/solution.py
@@ -12,7 +12,7 @@
 SMALL = 24
 CHUNKS = (12, 8, 6, 4)
 OFFSETS = (0, 12, 24, 20)
-GROUPS = (3, 2, 3, 2)
+GROUPS = (2, 2, 3, 2)
 
 
 def lane_index():
@@ -58,14 +58,12 @@
     return jnp.concatenate([tail, head, tail], axis=1)
 
 
-def stage_currents(currents, levels, held, lon):
-    tiles = lon // LANES + 1
-    for t in range(tiles):
-        for c in range(2):
-            for half in range(2):
-                pair = [natural_tile(currents, (c, 2 * half + k), t, lon) for k in range(2)]
-                held[pl.ds((t * 5 + 2 * c + half) * 8, 8), :] = jnp.concatenate(pair, axis=0)
-        column = natural_tile(levels, (), t, lon).astype(jnp.float32)
+def stage_flow(flow, held, lon):
+    for t in range(lon // LANES + 1):
+        for part in range(4):
+            pair = [natural_tile(flow, (2 * part + k,), t, lon) for k in range(2)]
+            held[pl.ds((t * 5 + part) * 8, 8), :] = jnp.concatenate(pair, axis=0)
+        column = natural_tile(flow, (8,), t, lon)
         held[pl.ds((t * 5 + 4) * 8, 8), :] = jnp.concatenate([column, column], axis=0)
 
 
@@ -107,23 +105,16 @@
 
 def pack_kernel(offset, n, lon, small, *refs):
     if small:
-        x_hbm, c_hbm, l_hbm, to_far, to_near, near_small, x, tail, sem, currents, levels, held, sems = refs
+        x, flow, to_far, to_near, near_small, tail, held = refs
     else:
-        x_hbm, to_far, to_near, x, tail, sem = refs
+        x, to_far, to_near, tail = refs
     full, rem = divmod(lon, LANES)
     size = (16 * full + 4) * n
     place = lax.axis_index("lat")
     top = place == lax.axis_size("lat") - 1
-    copy = pltpu.make_async_copy(x_hbm.at[pl.ds(offset, n)], x, sem)
     if small:
-        copies = [pltpu.make_async_copy(c_hbm, currents, sems.at[0]), pltpu.make_async_copy(l_hbm, levels, sems.at[1])]
-        for c in copies:
-            c.start()
-        copy.start()
         odd = place % 2 == 1
-        for c in copies:
-            c.wait()
-        stage_currents(currents, levels, held, lon)
+        stage_flow(flow, held, lon)
         edge_rows(held, near_small, 0, jnp.logical_not(odd), lon)
 
         @pl.when(jnp.logical_not(top))
@@ -133,9 +124,7 @@
         @pl.when(top)
         def _():
             folded_edge_rows(held, to_far, size, lon)
-    else:
-        copy.start()
-    copy.wait()
+
     lane = lane_index()
 
     def joined(rests):
@@ -149,9 +138,9 @@
         for k in range(2):
             for level in range(4):
                 for t in range(full):
-                    tile = x[2 * g + k, level, :, pl.ds(t * LANES, LANES)]
+                    tile = x[offset + 2 * g + k, level, :, pl.ds(t * LANES, LANES)]
                     to_near[pl.ds(first + t * 8 + 4 * k + level, 4, stride=full * 8), :] = tile
-                rest = x[2 * g + k, level, :, pl.ds(full * LANES, rem)]
+                rest = x[offset + 2 * g + k, level, :, pl.ds(full * LANES, rem)]
                 tail[pl.ds(4 * k + level, 4, stride=8), :] = jnp.concatenate([rest] * (LANES // rem), axis=1)
         end = pl.multiple_of(16 * full * n + 8 * g, 8)
         to_near[pl.ds(end, 8), :] = joined([tail[pl.ds(8 * r, 8), :] for r in range(4)])
@@ -180,14 +169,14 @@
     lax.fori_loop(0, n // 2, pair, 0)
 
 
-def coefficient_kernel(n, lon, currents, levels, near, far, k1, k2, held, u, v, w):
+def coefficient_kernel(n, lon, flow, near, far, k1, k2, held, u, v, w):
     full, _ = divmod(lon, LANES)
     tiles = full + 1
     far_base = (16 * full + 4) * n
     place = lax.axis_index("lat")
     odd = place % 2 == 1
     level = (lax.broadcasted_iota(jnp.int32, (8, LANES), 0) % 4).astype(jnp.float32)
-    stage_currents(currents, levels, held, lon)
+    stage_flow(flow, held, lon)
 
     def put(dst, row, t, value):
         dst[pl.ds((row * tiles + t) * 8, 8), :] = value
@@ -352,6 +341,8 @@
     f32 = jnp.float32
 
     packed, kept, near_small = [], [], None
+    merged = currents.reshape(2 * levels, rows, lon)
+    flow = jnp.concatenate([merged, column_levels.astype(f32)[None]], axis=0)
     for i, (offset, n) in enumerate(zip(OFFSETS, CHUNKS)):
         small = i == 0
         size = (16 * full + 4) * n
@@ -359,24 +350,19 @@
             jax.ShapeDtypeStruct((size + (SMALL * tiles if small else 0), LANES), f32),
             jax.ShapeDtypeStruct((size, LANES), f32),
         ]
-        scratch = [pltpu.VMEM((n, levels, rows, lon), f32), pltpu.VMEM((32, LANES), f32), pltpu.SemaphoreType.DMA]
+        scratch = [pltpu.VMEM((32, LANES), f32)]
         if small:
             shape.append(jax.ShapeDtypeStruct((SMALL * tiles, LANES), f32))
-            scratch += [
-                pltpu.VMEM(currents.shape, f32),
-                pltpu.VMEM(column_levels.shape, jnp.int32),
-                pltpu.VMEM((tiles * 40, LANES), f32),
-                pltpu.SemaphoreType.DMA((2,)),
-            ]
+            scratch.append(pltpu.VMEM((tiles * 40, LANES), f32))
         result = pl.pallas_call(
             functools.partial(pack_kernel, offset, n, lon, small),
             out_shape=shape,
-            in_specs=[pl.BlockSpec(memory_space=pltpu.HBM)] * (3 if small else 1),
+            in_specs=[vmem()] * (2 if small else 1),
             out_specs=[vmem() for _ in shape],
             scratch_shapes=scratch,
             cost_estimate=pl.CostEstimate(flops=1000000 * n, bytes_accessed=n * 184320, transcendentals=0),
             compiler_params=pltpu.CompilerParams(vmem_limit_bytes=16 * 2**20),
-        )(tracers, *((currents, column_levels) if small else ()))
+        )(tracers, *((flow,) if small else ()))
         packed.append(result[0])
         kept.append(result[1])
         if small:
@@ -394,7 +380,7 @@
             jax.ShapeDtypeStruct((8 * tiles * 9 * 8, LANES), f32),
             jax.ShapeDtypeStruct((4 * tiles * 10 * 8, LANES), f32),
         ],
-        in_specs=[vmem()] * 4,
+        in_specs=[vmem()] * 3,
         out_specs=[vmem()] * 2,
         scratch_shapes=[
             pltpu.VMEM((tiles * 40, LANES), f32),
@@ -405,7 +391,7 @@
         cost_estimate=pl.CostEstimate(flops=8000000, bytes_accessed=6000000, transcendentals=0),
         compiler_params=pltpu.CompilerParams(vmem_limit_bytes=20 * 2**20),
         name="coefficients",
-    )(currents, column_levels, small_received, far[0])
+    )(flow, small_received, far[0])
     out = None
     for i, (offset, n, groups) in enumerate(zip(OFFSETS, CHUNKS, GROUPS)):
         operands = [kept[i], near[i], far[i], k1, k2]

time: 57.8 us -> 56.4 us (0.976)
  other arithmetic: 0 us -> 1.72 us
  local copies, waits for them, and re-layouts: 3.51 us -> 1.83 us
  Pallas kernels: 23 us -> 21.6 us
    unnamed x10 -> x2, local copies, waits for them, and re-layouts: 3.51 us -> 1.83 us
    concatenate x0 -> x1, other arithmetic: none -> 0.98 us  [shards(): flow = jnp.concatenate([merged, column_levels.astype(f32)[None]], axis=0)]
    pallas_call x4, Pallas kernels: 2.89 us -> 1.99 us  [shards(): pl.pallas_call(functools.partial(pack_kernel, offset, n, lon, small), out...]
    broadcast_in_dim x0 -> x1, other arithmetic: none -> 0.74 us  [shards(): flow = jnp.concatenate([merged, column_levels.astype(f32)[None]], axis=0)]
  transfers between devices with their start and end apart: 9 -> 9, of which waited for: 1 -> 1; matrix products, arithmetic and copies ran while one was open for 0% -> 0% of each run, Pallas kernels for 33% -> 32%
where the time goes in v3:
time: 56.4 us; the launch traced here: 56.2 us
  starting transfers between devices  29.9 us (53%)
  Pallas kernels  21.6 us (38%)
  local copies, waits for them, and re-layouts  1.83 us (3%)
  other arithmetic  1.72 us (3%)
  waiting for transfers between devices  0.98 us (2%)
    pallas_call x4, Pallas kernels, shards(): pl.pallas_call(functools.partial(advect_kernel, n, lon, groups), out_shap...  18.1 us
    ppermute x4, starting transfers between devices, shards(): near.append(lax.ppermute(kept[i], 'lat', near_pairs))  17.1 us
    ppermute x4, starting transfers between devices, shards(): far.append(lax.ppermute(packed[i], 'lat', far_pairs))  12.7 us
    pallas_call x4, Pallas kernels, shards(): pl.pallas_call(functools.partial(pack_kernel, offset, n, lon, small), out...  1.99 us
    unnamed x2, local copies, waits for them, and re-layouts  1.83 us
    pallas_call x1, Pallas kernels, shards(): pl.pallas_call(functools.partial(coefficient_kernel, CHUNKS[0], lon), out...  1.45 us
  transfers between devices with their start and end apart: 9, of which 1 were waited for; matrix products, arithmetic and copies ran while one was open for 0% of the time, Pallas kernels for 32%

profile of v3, /device:TPU:33, one launch (start us, length us, event | category | flops | bytes accessed | tf_op | source)
XLA Modules:
  0.0 56.2 jit_solution(11733457240434853112)
XLA Ops:
  0.0 0.7 %convert_bitcast_fusion = f32[1,4,1440]{2,1,0:T(4,128)S(1)} fusion(s32[4,1440]{1,0:T(4,128)} %param.5), kind=kLoop, calls=%fused_computation.1 | loop fusion | flops 5760 | bytes 46080 | tf_op jit(solution)/shard_map/broadcast_in_dim | solution.py:345
  0.7 1.0 %pad_maximum_fusion.refs_1_.flow = f32[9,4,1440]{2,1,0:T(4,128)S(1)} fusion(f32[1,4,1440]{2,1,0:T(4,128)S(1)} %convert_bitcast_fusion, f32[8,4,1440]{2,1,0:T(4,128)} %bitcast.3), kind=kLoop, calls=%fused_computation | loop fusion | flops 51840 | bytes 414720 | tf_op jit(solution)/shard_map/concatenate | solution.py:345
  1.7 0.0 copy-start
  1.7 1.8 %copy-done = f32[30,4,4,1440]{3,2,1,0:T(4,128)S(1)} copy-done((f32[30,4,4,1440]{3,2,1,0:T(4,128)S(1)}, f32[30,4,4,1440]{3,2,1,0:T(4,128)}, u32[]{:S(2)}) %copy-start) | copy-done | bytes 2764824
  3.6 0.9 %shard_map.38 = (f32[2448,128]{1,0:T(8,128)S(1)}, f32[2160,128]{1,0:T(8,128)S(1)}, f32[288,128]{1,0:T(8,128)S(1)}) custom-call(f32[30,4,4,1440]{3,2,1,0:T(4,128)S(1)} %copy-done, f32[9,4,1440]{2,1,0:T(4,128)S(1)} %pad_maximum_fusion.refs_1_.flow), custom_call_target="tpu_custom_call" | custom-call | flops 12000000 | bytes 2211840 | tf_op jit(solution)/shard_map/pallas_call | solution.py:357
  4.4 4.6 %collective-permute-start.3 = (f32[2448,128]{1,0:T(8,128)S(1)}, f32[2448,128]{1,0:T(8,128)S(1)}, u32[]{:S(2)}, u32[]{:S(2)}) collective-permute-start(f32[2448,128]{1,0:T(8,128)S(1)} %get-tuple-element.19), channel_id=1, source_target_pairs={{1,2},{2,1},{3,4},{4,3},{5,6},{6,5},{7,8},{8,7},{9,10},{10,9},{11,... | collective-permute-start | bytes 3760136 | tf_op jit(solution)/shard_map/ppermute | solution.py:372
  9.0 16.7 %collective-permute-start.8 = (f32[2160,128]{1,0:T(8,128)S(1)}, f32[2160,128]{1,0:T(8,128)S(1)}, u32[]{:S(2)}, u32[]{:S(2)}) collective-permute-start(f32[2160,128]{1,0:T(8,128)S(1)} %get-tuple-element.26.own), channel_id=1, source_target_pairs={{0,1},{1,0},{2,3},{3,2},{4,5},{5,4},{6,7},{7,6},{8,9},{9,8},{10,11... | collective-permute-start | bytes 3317768 | tf_op jit(solution)/shard_map/ppermute | solution.py:376
  25.7 0.5 shard_map.40
  26.2 0.2 collective-permute-start.6
  26.4 1.9 %collective-permute-start.7 = (f32[1440,128]{1,0:T(8,128)S(1)}, f32[1440,128]{1,0:T(8,128)S(1)}, u32[]{:S(2)}, u32[]{:S(2)}) collective-permute-start(f32[1440,128]{1,0:T(8,128)S(1)} %get-tuple-element.25), channel_id=1, source_target_pairs={{1,2},{2,1},{3,4},{4,3},{5,6},{6,5},{7,8},{8,7},{9,10},{10,9},{11,... | collective-permute-start | bytes 2211848 | tf_op jit(solution)/shard_map/ppermute | solution.py:372
  28.3 0.1 collective-permute-start.2
  28.5 0.4 shard_map.39
  28.9 1.0 %collective-permute-done.2.near = f32[288,128]{1,0:T(8,128)S(1)} collective-permute-done((f32[288,128]{1,0:T(8,128)S(1)}, f32[288,128]{1,0:T(8,128)S(1)}, u32[]{:S(2)}, u32[]{:S(2)}) %collective-permute-start.2) | collective-permute-done | bytes 147488 | tf_op jit(solution)/shard_map/ppermute | solution.py:373
  29.8 0.1 collective-permute-start.4
  30.0 0.0 collective-permute-done.6.near
  30.0 3.7 %collective-permute-start.5 = (f32[1080,128]{1,0:T(8,128)S(1)}, f32[1080,128]{1,0:T(8,128)S(1)}, u32[]{:S(2)}, u32[]{:S(2)}) collective-permute-start(f32[1080,128]{1,0:T(8,128)S(1)} %get-tuple-element.23), channel_id=1, source_target_pairs={{1,2},{2,1},{3,4},{4,3},{5,6},{6,5},{7,8},{8,7},{9,10},{10,9},{11,... | collective-permute-start | bytes 1658888 | tf_op jit(solution)/shard_map/ppermute | solution.py:372
  33.6 0.3 shard_map.37
  33.9 0.0 collective-permute-done.8.near
  33.9 0.1 collective-permute-start
  34.1 0.0 collective-permute-done.3.far
  34.1 2.5 %collective-permute-start.1 = (f32[720,128]{1,0:T(8,128)S(1)}, f32[720,128]{1,0:T(8,128)S(1)}, u32[]{:S(2)}, u32[]{:S(2)}) collective-permute-start(f32[720,128]{1,0:T(8,128)S(1)} %get-tuple-element.17), channel_id=1, source_target_pairs={{1,2},{2,1},{3,4},{4,3},{5,6},{6,5},{7,8},{8,7},{9,10},{10,9},{11,... | collective-permute-start | bytes 1105928 | tf_op jit(solution)/shard_map/ppermute | solution.py:372
  36.5 1.5 %coefficients.1 = (f32[6912,128]{1,0:T(8,128)S(1)}, f32[3840,128]{1,0:T(8,128)S(1)}) custom-call(f32[9,4,1440]{2,1,0:T(4,128)S(1)} %pad_maximum_fusion.refs_1_.flow, f32[288,128]{1,0:T(8,128)S(1)} %collective-permute-done.2.near, f32[2448,128]{1,0:T(8,128)S(1)} %collective-permute-done.3.far), custom_call_target="tpu_custom_call" | custom-call | flops 8000000 | bytes 6000000 | tf_op jit(solution)/shard_map/coefficients/pallas_call | solution.py:377
  38.0 6.7 %shard_map.41.refs_0_ = f32[30,4,4,1440]{3,2,1,0:T(4,128)} custom-call(f32[2160,128]{1,0:T(8,128)S(1)} %get-tuple-element.26.own, f32[2160,128]{1,0:T(8,128)S(1)} %collective-permute-done.8.near, f32[2448,128]{1,0:T(8,128)S(1)} %collective-permute-done.3.far, f32[6912,128]{1,0:T(8,128)S(1)} %get-tuple-element.20.k1, f32[3840,128]{1,0:T(8,128)S(1)} %get-tuple-element.21.k2), custom_call_target="tpu_custom_call" | custom-call | flops 36000000 | bytes 6000000 | tf_op jit(solution)/shard_map/pallas_call | solution.py:404
  44.7 0.0 collective-permute-done.7.far
  44.7 4.7 %shard_map.42.refs_0_ = f32[30,4,4,1440]{3,2,1,0:T(4,128)} custom-call(f32[1440,128]{1,0:T(8,128)S(1)} %get-tuple-element.24.own, f32[1440,128]{1,0:T(8,128)S(1)} %collective-permute-done.6.near, f32[1440,128]{1,0:T(8,128)S(1)} %collective-permute-done.7.far, f32[6912,128]{1,0:T(8,128)S(1)} %get-tuple-element.20.k1, ...), custom_call_target="tpu_custom_call", output_to_operand_aliasing={{}: (5, {})} | custom-call | flops 24000000 | bytes 4000000 | tf_op jit(solution)/shard_map/pallas_call | solution.py:404
  49.4 0.0 collective-permute-done.4.near
  49.4 0.0 collective-permute-done.5.far
  49.4 4.0 %shard_map.43.refs_0_ = f32[30,4,4,1440]{3,2,1,0:T(4,128)} custom-call(f32[1080,128]{1,0:T(8,128)S(1)} %get-tuple-element.22.own, f32[1080,128]{1,0:T(8,128)S(1)} %collective-permute-done.4.near, f32[1080,128]{1,0:T(8,128)S(1)} %collective-permute-done.5.far, f32[6912,128]{1,0:T(8,128)S(1)} %get-tuple-element.20.k1, ...), custom_call_target="tpu_custom_call", output_to_operand_aliasing={{}: (5, {})} | custom-call | flops 18000000 | bytes 3000000 | tf_op jit(solution)/shard_map/pallas_call | solution.py:404
  53.4 0.0 collective-permute-done.near
  53.4 0.0 collective-permute-done.1.far
  53.5 2.7 %shard_map.44 = f32[30,4,4,1440]{3,2,1,0:T(4,128)} custom-call(f32[720,128]{1,0:T(8,128)S(1)} %get-tuple-element.16.own, f32[720,128]{1,0:T(8,128)S(1)} %collective-permute-done.near, f32[720,128]{1,0:T(8,128)S(1)} %collective-permute-done.1.far, f32[6912,128]{1,0:T(8,128)S(1)} %get-tuple-element.20.k1, ...), custom_call_target="tpu_custom_call", output_to_operand_aliasing={{}: (5, {})} | custom-call | flops 12000000 | bytes 2000000 | tf_op jit(solution)/shard_map/pallas_call | solution.py:404
Async XLA Ops:
  1.7 1.8 %copy-start = (f32[30,4,4,1440]{3,2,1,0:T(4,128)S(1)}, f32[30,4,4,1440]{3,2,1,0:T(4,128)}, u32[]{:S(2)}) copy-start(f32[30,4,4,1440]{3,2,1,0:T(4,128)} %refs_0_.7) | copy-start | bytes 8294404
  4.4 29.6 %collective-permute-start.3 = (f32[2448,128]{1,0:T(8,128)S(1)}, f32[2448,128]{1,0:T(8,128)S(1)}, u32[]{:S(2)}, u32[]{:S(2)}) collective-permute-start(f32[2448,128]{1,0:T(8,128)S(1)} %get-tuple-element.19), channel_id=1, source_target_pairs={{1,2},{2,1},{3,4},{4,3},{5,6},{6,5},{7,8},{8,7},{9,10},{10,9},{11,... | collective-permute-start | bytes 3760136 | tf_op jit(solution)/shard_map/ppermute | solution.py:372
  9.0 24.9 %collective-permute-start.8 = (f32[2160,128]{1,0:T(8,128)S(1)}, f32[2160,128]{1,0:T(8,128)S(1)}, u32[]{:S(2)}, u32[]{:S(2)}) collective-permute-start(f32[2160,128]{1,0:T(8,128)S(1)} %get-tuple-element.26.own), channel_id=1, source_target_pairs={{0,1},{1,0},{2,3},{3,2},{4,5},{5,4},{6,7},{7,6},{8,9},{9,8},{10,11... | collective-permute-start | bytes 3317768 | tf_op jit(solution)/shard_map/ppermute | solution.py:376
  26.2 3.8 %collective-permute-start.6 = (f32[1440,128]{1,0:T(8,128)S(1)}, f32[1440,128]{1,0:T(8,128)S(1)}, u32[]{:S(2)}, u32[]{:S(2)}) collective-permute-start(f32[1440,128]{1,0:T(8,128)S(1)} %get-tuple-element.24.own), channel_id=1, source_target_pairs={{0,1},{1,0},{2,3},{3,2},{4,5},{5,4},{6,7},{7,6},{8,9},{9,8},{10,11... | collective-permute-start | bytes 2211848 | tf_op jit(solution)/shard_map/ppermute | solution.py:376
  26.4 18.4 %collective-permute-start.7 = (f32[1440,128]{1,0:T(8,128)S(1)}, f32[1440,128]{1,0:T(8,128)S(1)}, u32[]{:S(2)}, u32[]{:S(2)}) collective-permute-start(f32[1440,128]{1,0:T(8,128)S(1)} %get-tuple-element.25), channel_id=1, source_target_pairs={{1,2},{2,1},{3,4},{4,3},{5,6},{6,5},{7,8},{8,7},{9,10},{10,9},{11,... | collective-permute-start | bytes 2211848 | tf_op jit(solution)/shard_map/ppermute | solution.py:372
  28.3 1.5 %collective-permute-start.2 = (f32[288,128]{1,0:T(8,128)S(1)}, f32[288,128]{1,0:T(8,128)S(1)}, u32[]{:S(2)}, u32[]{:S(2)}) collective-permute-start(f32[288,128]{1,0:T(8,128)S(1)} %get-tuple-element.18), channel_id=1, source_target_pairs={{0,1},{1,0},{2,3},{3,2},{4,5},{5,4},{6,7},{7,6},{8,9},{9,8},{10,11... | collective-permute-start | bytes 442376 | tf_op jit(solution)/shard_map/ppermute | solution.py:373
  29.8 19.6 %collective-permute-start.4 = (f32[1080,128]{1,0:T(8,128)S(1)}, f32[1080,128]{1,0:T(8,128)S(1)}, u32[]{:S(2)}, u32[]{:S(2)}) collective-permute-start(f32[1080,128]{1,0:T(8,128)S(1)} %get-tuple-element.22.own), channel_id=1, source_target_pairs={{0,1},{1,0},{2,3},{3,2},{4,5},{5,4},{6,7},{7,6},{8,9},{9,8},{10,11... | collective-permute-start | bytes 1658888 | tf_op jit(solution)/shard_map/ppermute | solution.py:376
  30.0 19.5 %collective-permute-start.5 = (f32[1080,128]{1,0:T(8,128)S(1)}, f32[1080,128]{1,0:T(8,128)S(1)}, u32[]{:S(2)}, u32[]{:S(2)}) collective-permute-start(f32[1080,128]{1,0:T(8,128)S(1)} %get-tuple-element.23), channel_id=1, source_target_pairs={{1,2},{2,1},{3,4},{4,3},{5,6},{6,5},{7,8},{8,7},{9,10},{10,9},{11,... | collective-permute-start | bytes 1658888 | tf_op jit(solution)/shard_map/ppermute | solution.py:372
  33.9 19.5 %collective-permute-start = (f32[720,128]{1,0:T(8,128)S(1)}, f32[720,128]{1,0:T(8,128)S(1)}, u32[]{:S(2)}, u32[]{:S(2)}) collective-permute-start(f32[720,128]{1,0:T(8,128)S(1)} %get-tuple-element.16.own), channel_id=1, source_target_pairs={{0,1},{1,0},{2,3},{3,2},{4,5},{5,4},{6,7},{7,6},{8,9},{9,8},{10,11... | collective-permute-start | bytes 1105928 | tf_op jit(solution)/shard_map/ppermute | solution.py:376
  34.1 19.4 %collective-permute-start.1 = (f32[720,128]{1,0:T(8,128)S(1)}, f32[720,128]{1,0:T(8,128)S(1)}, u32[]{:S(2)}, u32[]{:S(2)}) collective-permute-start(f32[720,128]{1,0:T(8,128)S(1)} %get-tuple-element.17), channel_id=1, source_target_pairs={{1,2},{2,1},{3,4},{4,3},{5,6},{6,5},{7,8},{8,7},{9,10},{10,9},{11,... | collective-permute-start | bytes 1105928 | tf_op jit(solution)/shard_map/ppermute | solution.py:372

commit v4 on v3

--- a/solution.py
+++ b/solution.py
@@ -10,8 +10,8 @@
 
 LANES = 128
 SMALL = 24
-CHUNKS = (12, 8, 6, 4)
-OFFSETS = (0, 12, 24, 20)
+CHUNKS = (8, 12, 6, 4)
+OFFSETS = (0, 8, 24, 20)
 GROUPS = (2, 2, 3, 2)
 
 
@@ -58,12 +58,12 @@
     return jnp.concatenate([tail, head, tail], axis=1)
 
 
-def stage_flow(flow, held, lon):
+def stage_flow(currents, levels, held, lon):
     for t in range(lon // LANES + 1):
         for part in range(4):
-            pair = [natural_tile(flow, (2 * part + k,), t, lon) for k in range(2)]
+            pair = [natural_tile(currents, (part // 2, 2 * (part % 2) + k), t, lon) for k in range(2)]
             held[pl.ds((t * 5 + part) * 8, 8), :] = jnp.concatenate(pair, axis=0)
-        column = natural_tile(flow, (8,), t, lon)
+        column = natural_tile(levels, (), t, lon).astype(jnp.float32)
         held[pl.ds((t * 5 + 4) * 8, 8), :] = jnp.concatenate([column, column], axis=0)
 
 
@@ -105,16 +105,24 @@
 
 def pack_kernel(offset, n, lon, small, *refs):
     if small:
-        x, flow, to_far, to_near, near_small, tail, held = refs
+        x_hbm, c_hbm, l_hbm, to_far, to_near, near_small, tail, held, x, currents, column, sems = refs
+        sources = ((x_hbm.at[pl.ds(offset, n)], x), (c_hbm, currents), (l_hbm, column))
+        copies = [pltpu.make_async_copy(a, b, sems.at[i]) for i, (a, b) in enumerate(sources)]
+        for copy in copies:
+            copy.start()
+        start = 0
     else:
         x, to_far, to_near, tail = refs
+        start = offset
     full, rem = divmod(lon, LANES)
     size = (16 * full + 4) * n
     place = lax.axis_index("lat")
     top = place == lax.axis_size("lat") - 1
     if small:
         odd = place % 2 == 1
-        stage_flow(flow, held, lon)
+        copies[1].wait()
+        copies[2].wait()
+        stage_flow(currents, column, held, lon)
         edge_rows(held, near_small, 0, jnp.logical_not(odd), lon)
 
         @pl.when(jnp.logical_not(top))
@@ -125,6 +133,7 @@
         def _():
             folded_edge_rows(held, to_far, size, lon)
 
+        copies[0].wait()
     lane = lane_index()
 
     def joined(rests):
@@ -138,9 +147,9 @@
         for k in range(2):
             for level in range(4):
                 for t in range(full):
-                    tile = x[offset + 2 * g + k, level, :, pl.ds(t * LANES, LANES)]
+                    tile = x[start + 2 * g + k, level, :, pl.ds(t * LANES, LANES)]
                     to_near[pl.ds(first + t * 8 + 4 * k + level, 4, stride=full * 8), :] = tile
-                rest = x[offset + 2 * g + k, level, :, pl.ds(full * LANES, rem)]
+                rest = x[start + 2 * g + k, level, :, pl.ds(full * LANES, rem)]
                 tail[pl.ds(4 * k + level, 4, stride=8), :] = jnp.concatenate([rest] * (LANES // rem), axis=1)
         end = pl.multiple_of(16 * full * n + 8 * g, 8)
         to_near[pl.ds(end, 8), :] = joined([tail[pl.ds(8 * r, 8), :] for r in range(4)])
@@ -169,14 +178,14 @@
     lax.fori_loop(0, n // 2, pair, 0)
 
 
-def coefficient_kernel(n, lon, flow, near, far, k1, k2, held, u, v, w):
+def coefficient_kernel(n, lon, currents, levels, near, far, k1, k2, held, u, v, w):
     full, _ = divmod(lon, LANES)
     tiles = full + 1
     far_base = (16 * full + 4) * n
     place = lax.axis_index("lat")
     odd = place % 2 == 1
     level = (lax.broadcasted_iota(jnp.int32, (8, LANES), 0) % 4).astype(jnp.float32)
-    stage_flow(flow, held, lon)
+    stage_flow(currents, levels, held, lon)
 
     def put(dst, row, t, value):
         dst[pl.ds((row * tiles + t) * 8, 8), :] = value
@@ -341,28 +350,32 @@
     f32 = jnp.float32
 
     packed, kept, near_small = [], [], None
-    merged = currents.reshape(2 * levels, rows, lon)
-    flow = jnp.concatenate([merged, column_levels.astype(f32)[None]], axis=0)
     for i, (offset, n) in enumerate(zip(OFFSETS, CHUNKS)):
         small = i == 0
         size = (16 * full + 4) * n
         shape = [
-            jax.ShapeDtypeStruct((size + (SMALL * tiles if small else 0), LANES), f32),
-            jax.ShapeDtypeStruct((size, LANES), f32),
+            pltpu.VMEM((size + (SMALL * tiles if small else 0), LANES), f32),
+            pltpu.VMEM((size, LANES), f32),
         ]
         scratch = [pltpu.VMEM((32, LANES), f32)]
         if small:
-            shape.append(jax.ShapeDtypeStruct((SMALL * tiles, LANES), f32))
-            scratch.append(pltpu.VMEM((tiles * 40, LANES), f32))
+            shape.append(pltpu.VMEM((SMALL * tiles, LANES), f32))
+            scratch += [
+                pltpu.VMEM((tiles * 40, LANES), f32),
+                pltpu.VMEM((n, levels, rows, lon), f32),
+                pltpu.VMEM(currents.shape, f32),
+                pltpu.VMEM(column_levels.shape, jnp.int32),
+                pltpu.SemaphoreType.DMA((3,)),
+            ]
         result = pl.pallas_call(
             functools.partial(pack_kernel, offset, n, lon, small),
             out_shape=shape,
-            in_specs=[vmem()] * (2 if small else 1),
+            in_specs=[pl.BlockSpec(memory_space=pltpu.HBM)] * 3 if small else [vmem()],
             out_specs=[vmem() for _ in shape],
             scratch_shapes=scratch,
             cost_estimate=pl.CostEstimate(flops=1000000 * n, bytes_accessed=n * 184320, transcendentals=0),
-            compiler_params=pltpu.CompilerParams(vmem_limit_bytes=16 * 2**20),
-        )(tracers, *((flow,) if small else ()))
+            compiler_params=pltpu.CompilerParams(vmem_limit_bytes=(56 if small else 16) * 2**20),
+        )(tracers, *((currents, column_levels) if small else ()))
         packed.append(result[0])
         kept.append(result[1])
         if small:
@@ -380,7 +393,7 @@
             jax.ShapeDtypeStruct((8 * tiles * 9 * 8, LANES), f32),
             jax.ShapeDtypeStruct((4 * tiles * 10 * 8, LANES), f32),
         ],
-        in_specs=[vmem()] * 3,
+        in_specs=[vmem()] * 4,
         out_specs=[vmem()] * 2,
         scratch_shapes=[
             pltpu.VMEM((tiles * 40, LANES), f32),
@@ -391,7 +404,7 @@
         cost_estimate=pl.CostEstimate(flops=8000000, bytes_accessed=6000000, transcendentals=0),
         compiler_params=pltpu.CompilerParams(vmem_limit_bytes=20 * 2**20),
         name="coefficients",
-    )(flow, small_received, far[0])
+    )(currents, column_levels, small_received, far[0])
     out = None
     for i, (offset, n, groups) in enumerate(zip(OFFSETS, CHUNKS, GROUPS)):
         operands = [kept[i], near[i], far[i], k1, k2]

time: 56.4 us -> 65 us (1.15)
  waiting for transfers between devices: 0.98 us -> 9.31 us
  other arithmetic: 1.72 us -> 0 us
  Pallas kernels: 21.6 us -> 22.8 us
  starting transfers between devices: 29.9 us -> 30.7 us
    ppermute x4, waiting for transfers between devices: 0.01 us -> 8.35 us  [shards(): far.append(lax.ppermute(packed[i], 'lat', far_pairs))]
    ppermute x4, starting transfers between devices: 17.1 us -> 20.8 us  [shards(): near.append(lax.ppermute(kept[i], 'lat', near_pairs))]
    ppermute x4, starting transfers between devices: 12.7 us -> 9.68 us  [shards(): far.append(lax.ppermute(packed[i], 'lat', far_pairs))]
    pallas_call x4, Pallas kernels: 1.99 us -> 3.18 us  [shards(): pl.pallas_call(functools.partial(pack_kernel, offset, n, lon, small), out...]
    concatenate x1 -> x0, other arithmetic: 0.98 us -> none  [shards(): flow = jnp.concatenate([merged, column_levels.astype(f32)[None]], axis=0)]
    broadcast_in_dim x1 -> x0, other arithmetic: 0.74 us -> none  [shards(): flow = jnp.concatenate([merged, column_levels.astype(f32)[None]], axis=0)]
    unnamed x2 -> x8, local copies, waits for them, and re-layouts: 1.83 us -> 1.85 us
  transfers between devices with their start and end apart: 9 -> 9, of which waited for: 1 -> 3; matrix products, arithmetic and copies ran while one was open for 0% -> 0% of each run, Pallas kernels for 32% -> 30%
where the time goes in v4:
time: 65 us; the launch traced here: 64.8 us
  starting transfers between devices  30.7 us (47%)
  Pallas kernels  22.8 us (35%)
  waiting for transfers between devices  9.31 us (14%)
  local copies, waits for them, and re-layouts  1.85 us (3%)
    ppermute x4, starting transfers between devices, shards(): near.append(lax.ppermute(kept[i], 'lat', near_pairs))  20.8 us
    pallas_call x4, Pallas kernels, shards(): pl.pallas_call(functools.partial(advect_kernel, n, lon, groups), out_shap...  18.2 us
    ppermute x4, starting transfers between devices, shards(): far.append(lax.ppermute(packed[i], 'lat', far_pairs))  9.68 us
    ppermute x4, waiting for transfers between devices, shards(): far.append(lax.ppermute(packed[i], 'lat', far_pairs))  8.35 us
    pallas_call x4, Pallas kernels, shards(): pl.pallas_call(functools.partial(pack_kernel, offset, n, lon, small), out...  3.18 us
    unnamed x8, local copies, waits for them, and re-layouts  1.85 us
    pallas_call x1, Pallas kernels, shards(): pl.pallas_call(functools.partial(coefficient_kernel, CHUNKS[0], lon), out...  1.45 us
  transfers between devices with their start and end apart: 9, of which 3 were waited for; matrix products, arithmetic and copies ran while one was open for 0% of the time, Pallas kernels for 30%

profile of v4, /device:TPU:33, one launch (start us, length us, event | category | flops | bytes accessed | tf_op | source)
XLA Modules:
  0.0 64.8 jit_solution(7655378782346013403)
XLA Ops:
  0.0 0.0 copy-start
  0.0 1.8 %copy-done = f32[30,4,4,1440]{3,2,1,0:T(4,128)S(1)} copy-done((f32[30,4,4,1440]{3,2,1,0:T(4,128)S(1)}, f32[30,4,4,1440]{3,2,1,0:T(4,128)}, u32[]{:S(2)}) %copy-start) | copy-done | bytes 2764824
  1.8 0.0 copy-start.1
  1.8 0.7 %shard_map.40 = (f32[2160,128]{1,0:T(8,128)S(1)}, f32[2160,128]{1,0:T(8,128)S(1)}) custom-call(f32[30,4,4,1440]{3,2,1,0:T(4,128)S(1)} %copy-done), custom_call_target="tpu_custom_call" | custom-call | flops 12000000 | bytes 2211840 | tf_op jit(solution)/shard_map/pallas_call | solution.py:370
  2.6 20.5 %collective-permute-start.6 = (f32[2160,128]{1,0:T(8,128)S(1)}, f32[2160,128]{1,0:T(8,128)S(1)}, u32[]{:S(2)}, u32[]{:S(2)}) collective-permute-start(f32[2160,128]{1,0:T(8,128)S(1)} %get-tuple-element.24.own), channel_id=1, source_target_pairs={{0,1},{1,0},{2,3},{3,2},{4,5},{5,4},{6,7},{7,6},{8,9},{9,8},{10,11... | collective-permute-start | bytes 3317768 | tf_op jit(solution)/shard_map/ppermute | solution.py:389
  23.1 1.8 %shard_map.38 = (f32[1728,128]{1,0:T(8,128)S(1)}, f32[1440,128]{1,0:T(8,128)S(1)}, f32[288,128]{1,0:T(8,128)S(1)}) custom-call(f32[30,4,4,1440]{3,2,1,0:T(4,128)} %refs_0_.7, f32[2,4,4,1440]{3,2,1,0:T(4,128)} %currents.1, s32[4,1440]{1,0:T(4,128)} %levels.1), custom_call_target="tpu_custom_call" | custom-call | flops 8000000 | bytes 1474560 | tf_op jit(solution)/shard_map/pallas_call | solution.py:370
  24.9 0.2 collective-permute-start.8
  25.1 1.9 %collective-permute-start.3 = (f32[1728,128]{1,0:T(8,128)S(1)}, f32[1728,128]{1,0:T(8,128)S(1)}, u32[]{:S(2)}, u32[]{:S(2)}) collective-permute-start(f32[1728,128]{1,0:T(8,128)S(1)} %get-tuple-element.19), channel_id=1, source_target_pairs={{1,2},{2,1},{3,4},{4,3},{5,6},{6,5},{7,8},{8,7},{9,10},{10,9},{11,... | collective-permute-start | bytes 2654216 | tf_op jit(solution)/shard_map/ppermute | solution.py:385
  27.0 3.7 %collective-permute-start.7 = (f32[2160,128]{1,0:T(8,128)S(1)}, f32[2160,128]{1,0:T(8,128)S(1)}, u32[]{:S(2)}, u32[]{:S(2)}) collective-permute-start(f32[2160,128]{1,0:T(8,128)S(1)} %get-tuple-element.25), channel_id=1, source_target_pairs={{1,2},{2,1},{3,4},{4,3},{5,6},{6,5},{7,8},{8,7},{9,10},{10,9},{11,... | collective-permute-start | bytes 3317768 | tf_op jit(solution)/shard_map/ppermute | solution.py:385
  30.7 0.0 copy-start.2
  30.7 0.0 copy-start.3
  30.7 0.1 collective-permute-start.2
  30.9 0.0 copy-done.1
  30.9 0.4 shard_map.39
  31.3 0.9 %collective-permute-done.2.near = f32[288,128]{1,0:T(8,128)S(1)} collective-permute-done((f32[288,128]{1,0:T(8,128)S(1)}, f32[288,128]{1,0:T(8,128)S(1)}, u32[]{:S(2)}, u32[]{:S(2)}) %collective-permute-start.2) | collective-permute-done | bytes 147488 | tf_op jit(solution)/shard_map/ppermute | solution.py:386
  32.2 0.1 collective-permute-start.4
  32.4 0.0 collective-permute-done.8.near
  32.4 1.9 %collective-permute-start.5 = (f32[1080,128]{1,0:T(8,128)S(1)}, f32[1080,128]{1,0:T(8,128)S(1)}, u32[]{:S(2)}, u32[]{:S(2)}) collective-permute-start(f32[1080,128]{1,0:T(8,128)S(1)} %get-tuple-element.23), channel_id=1, source_target_pairs={{1,2},{2,1},{3,4},{4,3},{5,6},{6,5},{7,8},{8,7},{9,10},{10,9},{11,... | collective-permute-start | bytes 1658888 | tf_op jit(solution)/shard_map/ppermute | solution.py:385
  34.3 0.3 shard_map.37
  34.6 4.9 %collective-permute-done.3.far = f32[1728,128]{1,0:T(8,128)S(1)} collective-permute-done((f32[1728,128]{1,0:T(8,128)S(1)}, f32[1728,128]{1,0:T(8,128)S(1)}, u32[]{:S(2)}, u32[]{:S(2)}) %collective-permute-start.3) | collective-permute-done | bytes 884768 | tf_op jit(solution)/shard_map/ppermute | solution.py:385
  39.5 0.0 collective-permute-start
  39.5 0.0 collective-permute-done.6.near
  39.5 2.1 %collective-permute-start.1 = (f32[720,128]{1,0:T(8,128)S(1)}, f32[720,128]{1,0:T(8,128)S(1)}, u32[]{:S(2)}, u32[]{:S(2)}) collective-permute-start(f32[720,128]{1,0:T(8,128)S(1)} %get-tuple-element.17), channel_id=1, source_target_pairs={{1,2},{2,1},{3,4},{4,3},{5,6},{6,5},{7,8},{8,7},{9,10},{10,9},{11,... | collective-permute-start | bytes 1105928 | tf_op jit(solution)/shard_map/ppermute | solution.py:385
  41.6 0.0 copy-done.2
  41.6 0.0 copy-done.3
  41.6 1.5 %coefficients.1 = (f32[6912,128]{1,0:T(8,128)S(1)}, f32[3840,128]{1,0:T(8,128)S(1)}) custom-call(f32[2,4,4,1440]{3,2,1,0:T(4,128)S(1)} %copy-done.2, s32[4,1440]{1,0:T(4,128)S(1)} %copy-done.3, f32[288,128]{1,0:T(8,128)S(1)} %collective-permute-done.2.near, f32[1728,128]{1,0:T(8,128)S(1)} %collective-permute-done.3.far), custom_call_target="tpu_custom_call" | custom-call | flops 8000000 | bytes 6000000 | tf_op jit(solution)/shard_map/coefficients/pallas_call | solution.py:390
  43.1 4.8 %shard_map.41.refs_0_ = f32[30,4,4,1440]{3,2,1,0:T(4,128)} custom-call(f32[1440,128]{1,0:T(8,128)S(1)} %get-tuple-element.26.own, f32[1440,128]{1,0:T(8,128)S(1)} %collective-permute-done.8.near, f32[1728,128]{1,0:T(8,128)S(1)} %collective-permute-done.3.far, f32[6912,128]{1,0:T(8,128)S(1)} %get-tuple-element.20.k1, f32[3840,128]{1,0:T(8,128)S(1)} %get-tuple-element.21.k2), custom_call_target="tpu_custom_call" | custom-call | flops 24000000 | bytes 4000000 | tf_op jit(solution)/shard_map/pallas_call | solution.py:417
  47.8 3.5 %collective-permute-done.7.far = f32[2160,128]{1,0:T(8,128)S(1)} collective-permute-done((f32[2160,128]{1,0:T(8,128)S(1)}, f32[2160,128]{1,0:T(8,128)S(1)}, u32[]{:S(2)}, u32[]{:S(2)}) %collective-permute-start.7) | collective-permute-done | bytes 1105952 | tf_op jit(solution)/shard_map/ppermute | solution.py:385
  51.3 6.7 %shard_map.42.refs_0_ = f32[30,4,4,1440]{3,2,1,0:T(4,128)} custom-call(f32[2160,128]{1,0:T(8,128)S(1)} %get-tuple-element.24.own, f32[2160,128]{1,0:T(8,128)S(1)} %collective-permute-done.6.near, f32[2160,128]{1,0:T(8,128)S(1)} %collective-permute-done.7.far, f32[6912,128]{1,0:T(8,128)S(1)} %get-tuple-element.20.k1, ...), custom_call_target="tpu_custom_call", output_to_operand_aliasing={{}: (5, {})} | custom-call | flops 36000000 | bytes 6000000 | tf_op jit(solution)/shard_map/pallas_call | solution.py:417
  58.0 0.0 collective-permute-done.4.near
  58.0 0.0 collective-permute-done.5.far
  58.0 4.0 %shard_map.43.refs_0_ = f32[30,4,4,1440]{3,2,1,0:T(4,128)} custom-call(f32[1080,128]{1,0:T(8,128)S(1)} %get-tuple-element.22.own, f32[1080,128]{1,0:T(8,128)S(1)} %collective-permute-done.4.near, f32[1080,128]{1,0:T(8,128)S(1)} %collective-permute-done.5.far, f32[6912,128]{1,0:T(8,128)S(1)} %get-tuple-element.20.k1, ...), custom_call_target="tpu_custom_call", output_to_operand_aliasing={{}: (5, {})} | custom-call | flops 18000000 | bytes 3000000 | tf_op jit(solution)/shard_map/pallas_call | solution.py:417
  62.0 0.0 collective-permute-done.near
  62.0 0.0 collective-permute-done.1.far
  62.0 2.7 %shard_map.44 = f32[30,4,4,1440]{3,2,1,0:T(4,128)} custom-call(f32[720,128]{1,0:T(8,128)S(1)} %get-tuple-element.16.own, f32[720,128]{1,0:T(8,128)S(1)} %collective-permute-done.near, f32[720,128]{1,0:T(8,128)S(1)} %collective-permute-done.1.far, f32[6912,128]{1,0:T(8,128)S(1)} %get-tuple-element.20.k1, ...), custom_call_target="tpu_custom_call", output_to_operand_aliasing={{}: (5, {})} | custom-call | flops 12000000 | bytes 2000000 | tf_op jit(solution)/shard_map/pallas_call | solution.py:417
Async XLA Ops:
  0.0 1.8 %copy-start = (f32[30,4,4,1440]{3,2,1,0:T(4,128)S(1)}, f32[30,4,4,1440]{3,2,1,0:T(4,128)}, u32[]{:S(2)}) copy-start(f32[30,4,4,1440]{3,2,1,0:T(4,128)} %refs_0_.7) | copy-start | bytes 8294404
  1.8 29.1 %copy-start.1 = (f32[30,4,4,1440]{3,2,1,0:T(4,128)S(1)}, f32[30,4,4,1440]{3,2,1,0:T(4,128)}, u32[]{:S(2)}) copy-start(f32[30,4,4,1440]{3,2,1,0:T(4,128)} %refs_0_.7) | copy-start | bytes 8294404
  2.6 36.9 %collective-permute-start.6 = (f32[2160,128]{1,0:T(8,128)S(1)}, f32[2160,128]{1,0:T(8,128)S(1)}, u32[]{:S(2)}, u32[]{:S(2)}) collective-permute-start(f32[2160,128]{1,0:T(8,128)S(1)} %get-tuple-element.24.own), channel_id=1, source_target_pairs={{0,1},{1,0},{2,3},{3,2},{4,5},{5,4},{6,7},{7,6},{8,9},{9,8},{10,11... | collective-permute-start | bytes 3317768 | tf_op jit(solution)/shard_map/ppermute | solution.py:389
  24.9 7.5 %collective-permute-start.8 = (f32[1440,128]{1,0:T(8,128)S(1)}, f32[1440,128]{1,0:T(8,128)S(1)}, u32[]{:S(2)}, u32[]{:S(2)}) collective-permute-start(f32[1440,128]{1,0:T(8,128)S(1)} %get-tuple-element.26.own), channel_id=1, source_target_pairs={{0,1},{1,0},{2,3},{3,2},{4,5},{5,4},{6,7},{7,6},{8,9},{9,8},{10,11... | collective-permute-start | bytes 2211848 | tf_op jit(solution)/shard_map/ppermute | solution.py:389
  25.1 14.4 %collective-permute-start.3 = (f32[1728,128]{1,0:T(8,128)S(1)}, f32[1728,128]{1,0:T(8,128)S(1)}, u32[]{:S(2)}, u32[]{:S(2)}) collective-permute-start(f32[1728,128]{1,0:T(8,128)S(1)} %get-tuple-element.19), channel_id=1, source_target_pairs={{1,2},{2,1},{3,4},{4,3},{5,6},{6,5},{7,8},{8,7},{9,10},{10,9},{11,... | collective-permute-start | bytes 2654216 | tf_op jit(solution)/shard_map/ppermute | solution.py:385
  27.0 24.3 %collective-permute-start.7 = (f32[2160,128]{1,0:T(8,128)S(1)}, f32[2160,128]{1,0:T(8,128)S(1)}, u32[]{:S(2)}, u32[]{:S(2)}) collective-permute-start(f32[2160,128]{1,0:T(8,128)S(1)} %get-tuple-element.25), channel_id=1, source_target_pairs={{1,2},{2,1},{3,4},{4,3},{5,6},{6,5},{7,8},{8,7},{9,10},{10,9},{11,... | collective-permute-start | bytes 3317768 | tf_op jit(solution)/shard_map/ppermute | solution.py:385
  30.7 10.9 %copy-start.2 = (f32[2,4,4,1440]{3,2,1,0:T(4,128)S(1)}, f32[2,4,4,1440]{3,2,1,0:T(4,128)}, u32[]{:S(2)}) copy-start(f32[2,4,4,1440]{3,2,1,0:T(4,128)} %currents.1) | copy-start | bytes 552964
  30.7 10.9 %copy-start.3 = (s32[4,1440]{1,0:T(4,128)S(1)}, s32[4,1440]{1,0:T(4,128)}, u32[]{:S(2)}) copy-start(s32[4,1440]{1,0:T(4,128)} %levels.1) | copy-start | bytes 69124
  30.7 1.5 %collective-permute-start.2 = (f32[288,128]{1,0:T(8,128)S(1)}, f32[288,128]{1,0:T(8,128)S(1)}, u32[]{:S(2)}, u32[]{:S(2)}) collective-permute-start(f32[288,128]{1,0:T(8,128)S(1)} %get-tuple-element.18), channel_id=1, source_target_pairs={{0,1},{1,0},{2,3},{3,2},{4,5},{5,4},{6,7},{7,6},{8,9},{9,8},{10,11... | collective-permute-start | bytes 442376 | tf_op jit(solution)/shard_map/ppermute | solution.py:386
  32.2 25.8 %collective-permute-start.4 = (f32[1080,128]{1,0:T(8,128)S(1)}, f32[1080,128]{1,0:T(8,128)S(1)}, u32[]{:S(2)}, u32[]{:S(2)}) collective-permute-start(f32[1080,128]{1,0:T(8,128)S(1)} %get-tuple-element.22.own), channel_id=1, source_target_pairs={{0,1},{1,0},{2,3},{3,2},{4,5},{5,4},{6,7},{7,6},{8,9},{9,8},{10,11... | collective-permute-start | bytes 1658888 | tf_op jit(solution)/shard_map/ppermute | solution.py:389
  32.4 25.6 %collective-permute-start.5 = (f32[1080,128]{1,0:T(8,128)S(1)}, f32[1080,128]{1,0:T(8,128)S(1)}, u32[]{:S(2)}, u32[]{:S(2)}) collective-permute-start(f32[1080,128]{1,0:T(8,128)S(1)} %get-tuple-element.23), channel_id=1, source_target_pairs={{1,2},{2,1},{3,4},{4,3},{5,6},{6,5},{7,8},{8,7},{9,10},{10,9},{11,... | collective-permute-start | bytes 1658888 | tf_op jit(solution)/shard_map/ppermute | solution.py:385
  39.5 22.6 %collective-permute-start = (f32[720,128]{1,0:T(8,128)S(1)}, f32[720,128]{1,0:T(8,128)S(1)}, u32[]{:S(2)}, u32[]{:S(2)}) collective-permute-start(f32[720,128]{1,0:T(8,128)S(1)} %get-tuple-element.16.own), channel_id=1, source_target_pairs={{0,1},{1,0},{2,3},{3,2},{4,5},{5,4},{6,7},{7,6},{8,9},{9,8},{10,11... | collective-permute-start | bytes 1105928 | tf_op jit(solution)/shard_map/ppermute | solution.py:389
  39.5 22.6 %collective-permute-start.1 = (f32[720,128]{1,0:T(8,128)S(1)}, f32[720,128]{1,0:T(8,128)S(1)}, u32[]{:S(2)}, u32[]{:S(2)}) collective-permute-start(f32[720,128]{1,0:T(8,128)S(1)} %get-tuple-element.17), channel_id=1, source_target_pairs={{1,2},{2,1},{3,4},{4,3},{5,6},{6,5},{7,8},{8,7},{9,10},{10,9},{11,... | collective-permute-start | bytes 1105928 | tf_op jit(solution)/shard_map/ppermute | solution.py:385
